TPU v7x, 64 devices: a 2x2x8 block of a 4x4x8 slice. The times are simulated.
64 devices in a mesh: dp: 4 (over x, y), ep: 16 (over z, core).
Axes of the slice: x: 2, y: 2, z: 8, core: 2. Of those that a mesh axis runs over, the one named last changes fastest.
The devices are a block of a 4x4x8 slice.
Arguments:
- hidden: bfloat16 [16384, 1024], P(('dp', 'ep')), parts along dimension 0
- w_gate: bfloat16 [32, 1024, 512], P('ep')
- w_up: bfloat16 [32, 1024, 512], P('ep')
- w_down: bfloat16 [32, 512, 1024], P('ep')
- w_router: bfloat16 [1024, 32], replicated
- slot_expert: int32 [192], P('dp'), parts along dimension 0
- topk_idx: int32 [16384, 8], P(('dp', 'ep')), parts along dimension 0
- topk_slot: int32 [16384, 8], P(('dp', 'ep')), parts along dimension 0
Outputs:
- output 1: bfloat16 [16384, 1024], P(('dp', 'ep')), parts along dimension 0
- output 2: bfloat16 [192, 1024, 512], P(('dp', 'ep')), parts along dimension 0
- output 3: bfloat16 [192, 1024, 512], P(('dp', 'ep')), parts along dimension 0
- output 4: bfloat16 [192, 512, 1024], P(('dp', 'ep')), parts along dimension 0
There are 4 independent parts. A program takes and returns all parts, laid end to end along the dimension named above; an argument that names none is the same for every part.
All inputs are finite; a program needn't handle non-finite values.
Results may differ from a plain program's by a relative error of at most 0.00789102.
Values are sent between devices in bfloat16 or wider.
A program may use at most 768 MiB of HBM per device.

v0:
```python
import jax
import jax.numpy as jnp
from jax import lax
from jax.sharding import PartitionSpec as P, NamedSharding

ROUTE_SCALE = 2.5


def gate_weights(hid_rows, w_router, topk_idx):
    logits = jnp.dot(hid_rows, w_router, preferred_element_type=jnp.float32)
    chosen = jax.nn.sigmoid(jnp.take_along_axis(logits, topk_idx, axis=1))
    return ROUTE_SCALE * chosen / jnp.sum(chosen, axis=1, keepdims=True)


def slot_capacity(group_tokens, top_k, experts, groups):
    return 2 * group_tokens * top_k // (experts + groups + 3 * (groups // 2))


def serve_pairs(all_hid, all_gates, pair_owner, num_owned, owner_cap, p_gate, p_up, p_down):
    num_tokens, hid_width = all_hid.shape
    top_k = all_gates.shape[1]
    num_pairs = num_tokens * top_k
    flat_owner = pair_owner.reshape(num_pairs)
    sorted_pairs = jnp.argsort(flat_owner * num_pairs + jnp.arange(num_pairs))
    counts = jax.ops.segment_sum(jnp.ones((num_pairs,), jnp.int32), flat_owner, num_segments=num_owned + 1)[:num_owned]
    starts = jnp.cumsum(counts) - counts
    slot_rank = jnp.arange(owner_cap)
    picked = sorted_pairs[jnp.minimum(starts[:, None] + slot_rank[None, :], num_pairs - 1)]
    pair_weight = jnp.where(slot_rank[None, :] < counts[:, None], all_gates.reshape(num_pairs)[picked], 0.0)
    tok_ids = picked // top_k
    rows_in = all_hid[tok_ids]
    act_a = jnp.einsum("sch,shi->sci", rows_in, p_gate, preferred_element_type=jnp.float32)
    act_b = jnp.einsum("sch,shi->sci", rows_in, p_up, preferred_element_type=jnp.float32)
    hidden_act = (jax.nn.silu(act_a) * act_b).astype(jnp.bfloat16)
    expert_out = jnp.einsum("sci,sih->sch", hidden_act, p_down, preferred_element_type=jnp.float32).astype(jnp.bfloat16)
    contrib = pair_weight[:, :, None] * expert_out
    return jax.ops.segment_sum(contrib.reshape(num_owned * owner_cap, hid_width), tok_ids.reshape(num_owned * owner_cap), num_segments=num_tokens)


def solution(mesh):
    groups = mesh.shape["ep"]
    tok_spec = P(("dp", "ep"), None)
    weight_spec = P("ep", None, None)
    slot_spec = P(("dp", "ep"), None, None)

    def local_block(hid_rows, w_gate, w_up, w_down, w_router, slot_expert, topk_idx, topk_slot):
        dev_index = lax.axis_index("ep")
        experts = w_router.shape[1]
        top_k = topk_idx.shape[1]
        per_dev = slot_expert.shape[0] // groups
        my_experts = lax.dynamic_slice_in_dim(slot_expert, dev_index * per_dev, per_dev)
        p_gate = jnp.take(lax.all_gather(w_gate, "ep", tiled=True), my_experts, axis=0)
        p_up = jnp.take(lax.all_gather(w_up, "ep", tiled=True), my_experts, axis=0)
        p_down = jnp.take(lax.all_gather(w_down, "ep", tiled=True), my_experts, axis=0)
        gates = gate_weights(hid_rows, w_router, topk_idx)
        all_hid = lax.all_gather(hid_rows, "ep", tiled=True)
        all_gates = lax.all_gather(gates, "ep", tiled=True)
        all_slot = lax.all_gather(topk_slot, "ep", tiled=True)
        local_slot = all_slot - dev_index * per_dev
        pair_owner = jnp.where((local_slot >= 0) & (local_slot < per_dev), local_slot, per_dev)
        slot_cap = slot_capacity(all_hid.shape[0], top_k, experts, groups)
        partial = serve_pairs(all_hid, all_gates, pair_owner, per_dev, slot_cap, p_gate, p_up, p_down)
        y_rows = lax.psum_scatter(partial, "ep", scatter_dimension=0, tiled=True)
        return y_rows.astype(jnp.bfloat16), p_gate, p_up, p_down

    return jax.shard_map(local_block, mesh=mesh, in_specs=(tok_spec, weight_spec, weight_spec, weight_spec, P(None, None), P("dp"), tok_spec, tok_spec), out_specs=(tok_spec, slot_spec, slot_spec, slot_spec), check_vma=False)
```

profile of v0, /device:TPU:21, one launch (start us, length us, event | category | flops | bytes accessed | tf_op | source)
XLA Modules:
  0.0 759.8 jit_solution(5627762709672718965)
XLA Ops:
  7.3 0.7 all-gather.5.cloned.1.call-update
  8.1 0.7 all-gather.11.cloned.1.call-update
  8.9 0.7 all-gather.9.cloned.1.call-update
  9.7 0.6 all-gather.7.cloned.1.call-update
  10.3 23.4 %all_gather.18 = s32[4096,8]{0,1:T(8,128)S(1)} all-gather(s32[256,8]{0,1:T(8,128)S(1)} %copy-done.7), channel_id=1, replica_groups=mesh['dp'=4,'ep'=16] {'ep'}, dimensions={0}, use_global_device_ids=true | all-gather | bytes 139264 | tf_op jit(solution)/shard_map/all_gather | solution.py:58
  33.8 0.6 copy.26
  34.4 1.0 mul.37
  35.4 0.6 copy.27
  36.0 1.0 reshape.329
  37.1 226.3 %scatter_custom_fusion = s32[4]{0:T(128)S(1)} fusion(s32[32768]{0:T(1024)S(1)} %reshape.329, s32[32768]{0:T(1024)S(1)} %broadcast.252, s32[]{:T(128)} %constant.43.clone.1), kind=kCustom, calls=%fused_computation.49 | custom fusion | flops 32768 | bytes 20 | tf_op jit(solution)/shard_map/scatter-add | solution.py:25
  264.3 16.8 %gather_fusion.4 = f32[2048]{0:T(1024)S(1)} fusion(f32[256,32]{0,1:T(8,128)S(1)} %fusion.14, s32[2048]{0:T(1024)S(1)} %reshape.321), kind=kCustom, calls=%fused_computation.6 | custom fusion | bytes 32768 | tf_op jit(solution)/shard_map/jit(take_along_axis)/gather | solution.py:11
  281.3 15.8 %all_gather.19 = f32[4096,8]{0,1:T(8,128)S(1)} all-gather(f32[256,8]{0,1:T(8,128)S(1)} %multiply_divide_fusion), channel_id=1, replica_groups=mesh['dp'=4,'ep'=16] {'ep'}, dimensions={0}, use_global_device_ids=true | all-gather | bytes 139264 | tf_op jit(solution)/shard_map/all_gather | solution.py:57
  297.1 0.6 copy.30
  297.7 1.0 reshape.271
  298.8 11.4 %sort.17 = (s32[32768]{0:T(1024)}, s32[32768]{0:T(1024)S(1)}) sort(s32[32768]{0:T(1024)S(1)} %iota_add_fusion, s32[32768]{0:T(1024)S(1)} %iota.18), dimensions={0}, to_apply=%region_0.1 | sort | flops 491520 | bytes 524288 | tf_op jit(solution)/shard_map/jit(argsort)/sort | solution.py:24
  310.2 14.6 %gather_fusion = s32[2730]{0:T(1024)S(1)} fusion(s32[32768]{0:T(1024)S(1)} %get-tuple-element.6, s32[3072]{0:T(1024)S(1)} %pad_clamp_fusion.2), kind=kCustom, calls=%fused_computation.2 | custom fusion | bytes 32760 | tf_op jit(solution)/shard_map/gather | solution.py:28
  325.0 14.6 %gather_fusion.1 = f32[2730]{0:T(1024)S(1)} fusion(f32[32768]{0:T(1024)S(1)} %reshape.271, s32[3072]{0:T(1024)S(1)} %pad_clamp_fusion.1), kind=kCustom, calls=%fused_computation.3 | custom fusion | bytes 32760 | tf_op jit(solution)/shard_map/gather | solution.py:29
  340.1 17.6 %gather_fusion.2 = bf16[2730,1024]{1,0:T(8,128)(2,1)} fusion(bf16[4096,1024]{1,0:T(8,128)(2,1)} %all-gather.5.cloned.1.call-done, s32[3072]{0:T(1024)S(1)} %pad_clamp_fusion), kind=kCustom, calls=%fused_computation.4 | custom fusion | bytes 11193000 | tf_op jit(solution)/shard_map/gather | solution.py:31
  357.7 6.3 reshape.306
  364.0 2.6 gather_fusion.3
  366.6 44.1 %all-gather.9.cloned.1.call-done = bf16[32,1024,512]{2,1,0:T(8,128)(2,1)} async-done(((bf16[2,1024,512]{2,1,0:T(8,128)(2,1)}), bf16[32,1024,512]{2,1,0:T(8,128)(2,1)}) %all-gather.9.cloned.1.call-update) | async-done | bytes 33554448 | tf_op jit(solution)/shard_map/all_gather | solution.py:53
  410.7 4.4 gather_fusion.6
  415.0 2.0 broadcast_select_fusion.2
  417.1 164.7 %all-gather.7.cloned.1.call-done = bf16[32,1024,512]{2,1,0:T(8,128)(2,1)} async-done(((bf16[2,1024,512]{2,1,0:T(8,128)(2,1)}), bf16[32,1024,512]{2,1,0:T(8,128)(2,1)}) %all-gather.7.cloned.1.call-update) | async-done | bytes 33554448 | tf_op jit(solution)/shard_map/all_gather | solution.py:52
  581.7 4.4 gather_fusion.5
  586.1 4.2 broadcast_select_fusion
  590.3 8.6 %fusion.15 = f32[3,910,512]{2,1,0:T(8,128)} fusion(bf16[3,910,1024]{2,1,0:T(8,128)(2,1)} %reshape.306, bf16[3,1024,512]{2,1,0:T(8,128)(2,1)S(1)} %get-tuple-element.16), kind=kOutput, calls=%fused_computation.56 | convolution fusion | flops 2862612480 | bytes 14327808 | tf_op jit(solution)/shard_map/sch,shi->sci/dot_general | solution.py:32
  598.9 12.7 %convert_multiply_fusion = f32[3,910,1024]{2,1,0:T(8,128)} fusion(f32[3,910]{1,0:T(4,128)S(1)} %fusion.6, bf16[3,512,1024]{2,1,0:T(8,128)(2,1)S(1)} %copy-done.3, f32[3,910,512]{2,1,0:T(8,128)} %fusion.15, bf16[3,910,1024]{2,1,0:T(8,128)(2,1)} %reshape.306, bf16[3,1024,512]{2,1,0:T(8,128)(2,1)} %get-tuple-element.15), kind=kOutput, calls=%fused_computation.9 | convolution fusion | flops 5741998080 | bytes 28666536 | tf_op jit(solution)/shard_map/sci,sih->sch/dot_general | solution.py:35
  611.7 9.6 %reshape.339 = f32[2730,1024]{1,0:T(8,128)} reshape(f32[3,910,1024]{2,1,0:T(8,128)} %convert_multiply_fusion) | data formatting | bytes 22364160 | tf_op jit(solution)/shard_map/reshape | solution.py:37
  621.3 34.4 %scatter_custom_fusion.1 = f32[4096,1024]{1,0:T(8,128)} fusion(s32[2730]{0:T(1024)S(1)} %fusion.8, f32[2730,1024]{1,0:T(8,128)} %reshape.339, f32[]{:T(128)} %constant.34.clone.1), kind=kCustom, calls=%fused_computation.10 | custom fusion | flops 2795520 | bytes 16777728 | tf_op jit(solution)/shard_map/scatter-add | solution.py:37
  655.7 95.0 %reduce-scatter.2.cloned.1.call-done = f32[256,1024]{1,0:T(8,128)} async-done(((f32[4096,1024]{1,0:T(8,128)}), f32[256,1024]{1,0:T(8,128)}) %reduce-scatter.2.cloned.1.call-update) | async-done | bytes 1048592 | tf_op jit(solution)/shard_map/reduce_scatter | solution.py:63
  750.7 2.1 convert_element_type.15
  (55 shorter events, 2.1 us)
Async XLA Ops:
  7.2 256.9 %copy-start = (bf16[1024,32]{0,1:T(8,128)(2,1)S(1)}, bf16[1024,32]{0,1:T(8,128)(2,1)}, u32[]{:S(2)}) copy-start(bf16[1024,32]{0,1:T(8,128)(2,1)} %param.14) | copy-start | bytes 196612
  7.2 3.1 copy-start.7
  7.2 332.9 %all-gather.5.cloned.1.call-start = ((), (), s32[]{:S(2)}) async-start(), calls=%async_computation.1 | async-start | bytes 8912896 | tf_op jit(solution)/shard_map/all_gather | solution.py:56
  8.0 356.0 %all-gather.11.cloned.1.call-start = ((), (), s32[]{:S(2)}) async-start(), calls=%async_computation.4 | async-start | bytes 35651584 | tf_op jit(solution)/shard_map/all_gather | solution.py:54
  8.8 401.9 %all-gather.9.cloned.1.call-start = ((), (), s32[]{:S(2)}) async-start(), calls=%async_computation.3 | async-start | bytes 35651584 | tf_op jit(solution)/shard_map/all_gather | solution.py:53
  9.6 254.2 %copy-start.6 = (s32[256,8]{0,1:T(8,128)S(1)}, s32[256,8]{0,1:T(8,128)}, u32[]{:S(2)}) copy-start(s32[256,8]{0,1:T(8,128)} %param.16) | copy-start | bytes 24580
  9.6 254.4 %copy-start.5 = (bf16[256,1024]{1,0:T(8,128)(2,1)S(1)}, bf16[256,1024]{1,0:T(8,128)(2,1)}, u32[]{:S(2)}) copy-start(bf16[256,1024]{1,0:T(8,128)(2,1)} %param.10) | copy-start | bytes 1572868
  9.6 572.1 %all-gather.7.cloned.1.call-start = ((), (), s32[]{:S(2)}) async-start(), calls=%async_computation.2 | async-start | bytes 35651584 | tf_op jit(solution)/shard_map/all_gather | solution.py:52
  10.3 740.4 %reduce-scatter.2.cloned.1.call-start = ((), (), s32[]{:S(2)}) async-start(), calls=%async_computation.5 | async-start | bytes 17825792 | tf_op jit(solution)/shard_map/reduce_scatter | solution.py:63
  325.0 14.9 %copy-start.8 = (s32[48]{0:T(128)S(1)}, s32[48]{0:T(128)}, u32[]{:S(2)}) copy-start(s32[48]{0:T(128)} %param.15) | copy-start | bytes 580
  417.1 169.1 %copy-start.2 = (bf16[3,1024,512]{2,1,0:T(8,128)(2,1)S(1)}, bf16[3,1024,512]{2,1,0:T(8,128)(2,1)}, u32[]{:S(2)}) copy-start(bf16[3,1024,512]{2,1,0:T(8,128)(2,1)} %gather_fusion.6) | copy-start | bytes 9437188
  590.3 8.6 %copy-start.4 = (bf16[3,1024,512]{2,1,0:T(8,128)(2,1)}, bf16[3,1024,512]{2,1,0:T(8,128)(2,1)S(1)}, u32[]{:S(2)}) copy-start(bf16[3,1024,512]{2,1,0:T(8,128)(2,1)S(1)} %get-tuple-element.16) | copy-start | bytes 9437188
  590.3 8.6 %copy-start.3 = (bf16[3,512,1024]{2,1,0:T(8,128)(2,1)S(1)}, bf16[3,512,1024]{2,1,0:T(8,128)(2,1)}, u32[]{:S(2)}) copy-start(bf16[3,512,1024]{2,1,0:T(8,128)(2,1)} %broadcast_select_fusion.2) | copy-start | bytes 9437188
  655.7 97.1 %copy-start.1 = (bf16[1024,32]{0,1:T(8,128)(2,1)S(1)}, bf16[1024,32]{0,1:T(8,128)(2,1)}, u32[]{:S(2)}) copy-start(bf16[1024,32]{0,1:T(8,128)(2,1)} %param.14) | copy-start | bytes 196612
Sparse Core Ops, SparseCore 0:
  9.7 57.8 all-gather.4
  69.2 169.4 all-gather.10
  240.4 170.2 all-gather.8
  412.1 169.5 all-gather.6
  655.8 94.8 reduce-scatter.1
where the time goes:
time: 765 us; the launch traced here: 760 us
  waiting for transfers between devices  307 us (40%)
  other arithmetic  281 us (37%)
  local copies, waits for them, and re-layouts  96.6 us (13%)
  blocking collectives  39.2 us (5%)
  matrix products  21.6 us (3%)
  between operations  14.5 us (2%)
    scatter-add x1, other arithmetic, serve_pairs(): jax.ops.segment_sum(jnp.ones((num_pairs,), jnp.int32), flat_owner, num_se...  226 us
    all_gather x1, waiting for transfers between devices, local_block(): lax.all_gather(w_gate, 'ep', tiled=True)  165 us
    reduce_scatter x1, waiting for transfers between devices, local_block(): y_rows = lax.psum_scatter(partial, 'ep', scatter_dimension=0, tiled=True)  95 us
    all_gather x1, waiting for transfers between devices, local_block(): p_up = jnp.take(lax.all_gather(w_up, 'ep', tiled=True), my_experts, axis=0)  44.1 us
    scatter-add x1, other arithmetic, serve_pairs(): jax.ops.segment_sum(contrib.reshape(num_owned * owner_cap, hid_width), to...  34.4 us
    gather x2, local copies, waits for them, and re-layouts, serve_pairs(): rows_in = all_hid[tok_ids]  23.9 us
    all_gather x1, blocking collectives, local_block(): all_slot = lax.all_gather(topk_slot, 'ep', tiled=True)  23.4 us
    gather x5, local copies, waits for them, and re-layouts, gate_weights(): chosen = jax.nn.sigmoid(jnp.take_along_axis(logits, topk_idx, axis=1))  17.2 us
  transfers between devices with their start and end apart: 5, of which 3 were waited for; matrix products, arithmetic and copies ran while one was open for 43% of the time, Pallas kernels for 0%

commit v1 on v0

v1 whole, which is shorter than its diff:
```python
import functools

import jax
import jax.numpy as jnp
from jax import lax
from jax.experimental import pallas as pl
from jax.experimental.pallas import tpu as pltpu
from jax.sharding import PartitionSpec as P

ROUTE_SCALE = 2.5
LANES = 128
TILE = 512


def experts_kernel(first_ref, x_ref, router_ref, gate_ref, up_ref, down_ref, out_ref):
    width = router_ref.shape[0]
    rows = x_ref[:, :width]
    chosen = x_ref[:, width:].astype(jnp.float32) > 0.5
    logits = jnp.dot(rows, router_ref[...], preferred_element_type=jnp.float32)
    gates = jnp.where(chosen, jax.nn.sigmoid(logits), 0.0)
    weights = ROUTE_SCALE * gates / jnp.sum(gates, axis=1, keepdims=True)
    lane = lax.broadcasted_iota(jnp.int32, weights.shape, 1)
    for i in range(gate_ref.shape[0]):
        mine = (lane == first_ref[0] + i) & chosen
        weight = jnp.sum(jnp.where(mine, weights, 0.0), axis=1, keepdims=True)
        served = jnp.sum(jnp.where(mine, 1.0, 0.0), axis=1, keepdims=True) > 0.5
        act_a = jnp.dot(rows, gate_ref[i], preferred_element_type=jnp.float32)
        act_b = jnp.dot(rows, up_ref[i], preferred_element_type=jnp.float32)
        hidden_act = (jax.nn.silu(act_a) * act_b).astype(jnp.bfloat16)
        expert_out = jnp.dot(hidden_act, down_ref[i], preferred_element_type=jnp.float32)
        contrib = jnp.where(served, weight * expert_out.astype(jnp.bfloat16).astype(jnp.float32), 0.0)
        if i == 0:
            out_ref[...] = contrib
        else:
            out_ref[...] += contrib


def apply_experts(first, tokens, router, w_gate, w_up, w_down):
    num_tokens, ext_width = tokens.shape
    experts, width, inter = w_gate.shape
    whole = lambda shape: pl.BlockSpec(shape, lambda t, *_: (0,) * len(shape))
    return pl.pallas_call(
        experts_kernel,
        grid_spec=pltpu.PrefetchScalarGridSpec(
            num_scalar_prefetch=1,
            grid=(num_tokens // TILE,),
            in_specs=[
                pl.BlockSpec((TILE, ext_width), lambda t, *_: (t, 0)),
                whole(router.shape), whole(w_gate.shape), whole(w_up.shape), whole(w_down.shape),
            ],
            out_specs=pl.BlockSpec((TILE, width), lambda t, *_: (t, 0)),
        ),
        out_shape=jax.ShapeDtypeStruct((num_tokens, width), jnp.float32),
        compiler_params=pltpu.CompilerParams(vmem_limit_bytes=48 * 1024 * 1024),
        cost_estimate=pl.CostEstimate(flops=6 * num_tokens * experts * width * inter, bytes_accessed=40 * 2**20, transcendentals=0),
        name="experts",
    )(first, tokens, router, w_gate, w_up, w_down)


def pick_kernel(table_ref, in_ref, out_ref):
    out_ref[...] = in_ref[...]


def pick_pieces(table, pieces):
    count = table.shape[0]
    block = (1,) + pieces.shape[1:]
    return pl.pallas_call(
        pick_kernel,
        grid_spec=pltpu.PrefetchScalarGridSpec(
            num_scalar_prefetch=1,
            grid=(count,),
            in_specs=[pl.BlockSpec(block, lambda i, table: (table[i], 0, 0))],
            out_specs=pl.BlockSpec(block, lambda i, table: (i, 0, 0)),
        ),
        out_shape=jax.ShapeDtypeStruct((count,) + pieces.shape[1:], pieces.dtype),
        name="pick",
    )(table, pieces)


def exchange_kernel(groups, picked_ref, out_ref, stage, local_sem, send_sem, recv_sem):
    me = lax.axis_index("dp")
    ep = lax.axis_index("ep")
    rows = picked_ref.shape[2]
    barrier = pltpu.get_barrier_semaphore()
    for k in range(1, groups):
        pl.semaphore_signal(barrier, inc=1, device_id=(lax.rem(me + k, groups), ep), device_id_type=pl.DeviceIdType.MESH)
    pl.semaphore_wait(barrier, groups - 1)
    place = pl.ds(pl.multiple_of(me * rows, rows), rows)
    copies = []
    for k in range(1, groups):
        peer = lax.rem(me + k, groups)
        copy = pltpu.make_async_remote_copy(
            src_ref=picked_ref.at[peer],
            dst_ref=out_ref.at[:, place, :],
            send_sem=send_sem.at[k],
            recv_sem=recv_sem.at[k],
            device_id=(peer, ep),
            device_id_type=pl.DeviceIdType.MESH,
        )
        copy.start()
        copies.append(copy)
    load = pltpu.make_async_copy(picked_ref.at[me], stage, local_sem.at[0])
    load.start()
    load.wait()
    store = pltpu.make_async_copy(stage, out_ref.at[:, place, :], local_sem.at[1])
    store.start()
    store.wait()
    for copy in copies:
        copy.wait()


def exchange(picked, groups, which):
    _, slots, rows, columns = picked.shape
    return pl.pallas_call(
        functools.partial(exchange_kernel, groups),
        out_shape=jax.ShapeDtypeStruct((slots, rows * groups, columns), picked.dtype),
        in_specs=[pl.BlockSpec(memory_space=pl.ANY)],
        out_specs=pl.BlockSpec(memory_space=pl.ANY),
        scratch_shapes=[
            pltpu.VMEM((slots, rows, columns), picked.dtype),
            pltpu.SemaphoreType.DMA((2,)),
            pltpu.SemaphoreType.DMA((groups,)),
            pltpu.SemaphoreType.DMA((groups,)),
        ],
        compiler_params=pltpu.CompilerParams(collective_id=which, has_side_effects=True),
        cost_estimate=pl.CostEstimate(flops=10**9, bytes_accessed=9 * 2**20, transcendentals=0),
        name="exchange",
    )(picked)


def solution(mesh):
    members = mesh.shape["ep"]
    groups = mesh.shape["dp"]
    tok_spec = P(("dp", "ep"), None)
    weight_spec = P("ep", None, None)
    slot_spec = P(("dp", "ep"), None, None)

    def local_block(hid_rows, w_gate, w_up, w_down, w_router, slot_expert, topk_idx, topk_slot):
        dp_index = lax.axis_index("dp")
        ep_index = lax.axis_index("ep")
        width, experts = w_router.shape
        per_dev = slot_expert.shape[0] // members

        chosen = jnp.any(topk_idx[:, :, None] == jnp.arange(LANES)[None, None, :], axis=1).astype(hid_rows.dtype)
        tokens = lax.all_gather(jnp.concatenate([hid_rows, chosen], axis=1), "ep", tiled=True)
        router = jnp.pad(w_router, ((0, 0), (0, LANES - experts)))
        first = (ep_index * w_gate.shape[0]).astype(jnp.int32).reshape(1)
        partial = apply_experts(first, tokens, router, w_gate, w_up, w_down)
        y_rows = lax.psum_scatter(partial, "ep", scatter_dimension=0, tiled=True)

        my_slots = lax.dynamic_slice_in_dim(slot_expert, ep_index * per_dev, per_dev)
        table = lax.all_gather(my_slots, "dp", tiled=True)

        def place(weight, which):
            rows = weight.shape[1] // groups
            piece = lax.dynamic_slice_in_dim(weight, dp_index * rows, rows, axis=1)
            pieces = lax.all_gather(piece, "ep", tiled=True)
            picked = pick_pieces(table, pieces).reshape(groups, per_dev, rows, weight.shape[2])
            return exchange(picked, groups, which)

        p_gate, p_up, p_down = place(w_gate, 0), place(w_up, 1), place(w_down, 2)
        return y_rows.astype(jnp.bfloat16), p_gate, p_up, p_down

    return jax.shard_map(local_block, mesh=mesh, in_specs=(tok_spec, weight_spec, weight_spec, weight_spec, P(None, None), P("dp"), tok_spec, tok_spec), out_specs=(tok_spec, slot_spec, slot_spec, slot_spec), check_vma=False)
```

time: 765 us -> 347 us (0.45)
  other arithmetic: 281 us -> 4.49 us
  waiting for transfers between devices: 307 us -> 129 us
  Pallas kernels: 0 us -> 173 us
  local copies, waits for them, and re-layouts: 96.6 us -> 17.5 us
  blocking collectives: 39.2 us -> 6.71 us
  matrix products: 21.6 us -> 0 us
    scatter-add x2 -> x0, other arithmetic: 261 us -> none  [the longest x1 226 us: serve_pairs(): jax.ops.segment_sum(jnp.ones((num_pairs,), jnp.int32), flat_owner, num_se...]
    pallas_call x0 -> x7, Pallas kernels: none -> 173 us  [the longest x3 111 us: exchange(): pl.pallas_call(functools.partial(exchange_kernel, groups), out_shape=jax....]
    all_gather x4, waiting for transfers between devices: 209 us -> 77.8 us  [the longest x1 56.1 us: local_block(): lax.all_gather(jnp.concatenate([hid_rows, chosen], axis=1), 'ep', tiled=T...]
    gather x14 -> x0, local copies, waits for them, and re-layouts: 81.8 us -> none  [the longest x2 23.9 us: serve_pairs(): rows_in = all_hid[tok_ids]]
    reduce_scatter x1, waiting for transfers between devices: 95 us -> 51.4 us  [local_block(): y_rows = lax.psum_scatter(partial, 'ep', scatter_dimension=0, tiled=True)]
    all_gather x2 -> x0, blocking collectives: 39.2 us -> none  [the longest x1 23.4 us: local_block(): all_slot = lax.all_gather(topk_slot, 'ep', tiled=True)]
    dot_general x3 -> x0, matrix products: 21.6 us -> none  [the longest x1 12.7 us: serve_pairs(): jnp.einsum('sci,sih->sch', hidden_act, p_down, preferred_element_type=jnp...]
    unnamed x18 -> x24, local copies, waits for them, and re-layouts: 0.05 us -> 11.6 us
  transfers between devices with their start and end apart: 5 -> 5, of which waited for: 3 -> 5; matrix products, arithmetic and copies ran while one was open for 43% -> 2% of each run, Pallas kernels for 0% -> 50%
where the time goes in v1:
time: 347 us; the launch traced here: 346 us
  Pallas kernels  173 us (50%)
  waiting for transfers between devices  129 us (37%)
  local copies, waits for them, and re-layouts  17.5 us (5%)
  between operations  14.6 us (4%)
  blocking collectives  6.71 us (2%)
  other arithmetic  4.49 us (1%)
    pallas_call x3, Pallas kernels, exchange(): pl.pallas_call(functools.partial(exchange_kernel, groups), out_shape=jax....  111 us
    all_gather x1, waiting for transfers between devices, local_block(): lax.all_gather(jnp.concatenate([hid_rows, chosen], axis=1), 'ep', tiled=T...  56.1 us
    reduce_scatter x1, waiting for transfers between devices, local_block(): y_rows = lax.psum_scatter(partial, 'ep', scatter_dimension=0, tiled=True)  51.4 us
    pallas_call x1, Pallas kernels, apply_experts(): pl.pallas_call(experts_kernel, grid_spec=pltpu.PrefetchScalarGridSpec(num...  36.3 us
    pallas_call x3, Pallas kernels, pick_pieces(): pl.pallas_call(pick_kernel, grid_spec=pltpu.PrefetchScalarGridSpec(num_sc...  25.8 us
    all_gather x3, waiting for transfers between devices, place(): pieces = lax.all_gather(piece, 'ep', tiled=True)  21.7 us
    unnamed x24, local copies, waits for them, and re-layouts  11.6 us
  transfers between devices with their start and end apart: 5, of which 5 were waited for; matrix products, arithmetic and copies ran while one was open for 2% of the time, Pallas kernels for 50%

profile of v1, /device:TPU:21, one launch (start us, length us, event | category | flops | bytes accessed | tf_op | source)
XLA Modules:
  0.0 346.2 jit_solution(8600948479420595753)
XLA Ops:
  7.2 0.8 copy.15
  8.1 0.4 fusion
  8.6 1.9 pad_maximum_fusion
  10.6 0.1 all-gather.7.cloned.1.call-start
  10.6 2.0 constant_dynamic-slice_fusion.2
  12.7 0.1 all-gather.9.cloned.1.call-start
  12.8 1.9 constant_dynamic-slice_fusion.1
  14.8 1.9 constant_dynamic-slice_fusion
  16.8 0.2 copy.16
  17.1 56.1 %all-gather.5.cloned.1.call-done.x_ref = bf16[4096,1152]{1,0:T(8,128)(2,1)} async-done(((bf16[256,1152]{1,0:T(8,128)(2,1)}), bf16[4096,1152]{1,0:T(8,128)(2,1)}) %all-gather.5.cloned.1.call-update) | async-done | bytes 9437200 | tf_op jit(solution)/shard_map/all_gather | solution.py:145
  73.2 1.6 copy-done.1
  74.8 36.3 %experts.1 = f32[4096,1024]{1,0:T(8,128)} custom-call(s32[1]{0:T(128)} %bitcast.first_ref, bf16[4096,1152]{1,0:T(8,128)(2,1)} %all-gather.5.cloned.1.call-done.x_ref, bf16[1024,128]{1,0:T(8,128)(2,1)S(1)} %pad.4.router_ref, bf16[2,1024,512]{2,1,0:T(8,128)(2,1)S(1)} %copy-done, bf16[2,1024,512]{2,1,0:T(8,128)(2,1)S(1)} %copy-done.1, ...), custom_call_target="tpu_custom_call" | custom-call | flops 25769803776 | bytes 41943040 | tf_op jit(solution)/shard_map/experts/pallas_call | solution.py:42
  111.1 0.6 copy-done.7
  111.7 0.6 dynamic-slice
  112.9 0.2 dynamic-slice_dynamic-update-slice_fusion
  113.1 6.7 %all-reduce.1.table_ref = s32[12]{0:T(128)} all-reduce(s32[12]{0:T(128)S(1)} %dynamic-slice_dynamic-update-slice_fusion), channel_id=1, replica_groups=mesh['dp'=4,'ep'=16] {'dp'}, use_global_device_ids=true, to_apply=%add.1 | all-reduce | flops 12 | bytes 96
  119.8 6.6 %all-gather.7.cloned.1.call-done.in_ref = bf16[32,256,512]{2,1,0:T(8,128)(2,1)} async-done(((bf16[2,256,512]{2,1,0:T(8,128)(2,1)}), bf16[32,256,512]{2,1,0:T(8,128)(2,1)}) %all-gather.7.cloned.1.call-update) | async-done | bytes 8388624 | tf_op jit(solution)/shard_map/all_gather | solution.py:157
  126.4 8.6 %pick.3 = bf16[12,256,512]{2,1,0:T(8,128)(2,1)} custom-call(s32[12]{0:T(128)} %all-reduce.1.table_ref, bf16[32,256,512]{2,1,0:T(8,128)(2,1)} %all-gather.7.cloned.1.call-done.in_ref), custom_call_target="tpu_custom_call" | custom-call | tf_op jit(solution)/shard_map/pick/pallas_call | solution.py:67
  135.0 37.1 %exchange.3 = bf16[3,1024,512]{2,1,0:T(8,128)(2,1)} custom-call(bf16[4,3,256,512]{3,2,1,0:T(8,128)(2,1)} %bitcast.6), custom_call_target="tpu_custom_call" | custom-call | flops 1000000000 | bytes 9437184 | tf_op jit(solution)/shard_map/exchange/pallas_call | solution.py:114
  172.1 7.6 %all-gather.9.cloned.1.call-done.in_ref = bf16[32,256,512]{2,1,0:T(8,128)(2,1)} async-done(((bf16[2,256,512]{2,1,0:T(8,128)(2,1)}), bf16[32,256,512]{2,1,0:T(8,128)(2,1)}) %all-gather.9.cloned.1.call-update) | async-done | bytes 8388624 | tf_op jit(solution)/shard_map/all_gather | solution.py:157
  179.7 8.6 %pick.4 = bf16[12,256,512]{2,1,0:T(8,128)(2,1)} custom-call(s32[12]{0:T(128)} %all-reduce.1.table_ref, bf16[32,256,512]{2,1,0:T(8,128)(2,1)} %all-gather.9.cloned.1.call-done.in_ref), custom_call_target="tpu_custom_call" | custom-call | tf_op jit(solution)/shard_map/pick/pallas_call | solution.py:67
  188.3 37.1 %exchange.4 = bf16[3,1024,512]{2,1,0:T(8,128)(2,1)} custom-call(bf16[4,3,256,512]{3,2,1,0:T(8,128)(2,1)} %bitcast.7), custom_call_target="tpu_custom_call" | custom-call | flops 1000000000 | bytes 9437184 | tf_op jit(solution)/shard_map/exchange/pallas_call | solution.py:114
  225.4 7.4 %all-gather.11.cloned.1.call-done.in_ref = bf16[32,128,1024]{2,1,0:T(8,128)(2,1)} async-done(((bf16[2,128,1024]{2,1,0:T(8,128)(2,1)}), bf16[32,128,1024]{2,1,0:T(8,128)(2,1)}) %all-gather.11.cloned.1.call-update) | async-done | bytes 8388624 | tf_op jit(solution)/shard_map/all_gather | solution.py:157
  232.8 8.6 %pick.5 = bf16[12,128,1024]{2,1,0:T(8,128)(2,1)} custom-call(s32[12]{0:T(128)} %all-reduce.1.table_ref, bf16[32,128,1024]{2,1,0:T(8,128)(2,1)} %all-gather.11.cloned.1.call-done.in_ref), custom_call_target="tpu_custom_call" | custom-call | tf_op jit(solution)/shard_map/pick/pallas_call | solution.py:67
  241.4 37.1 %exchange.5 = bf16[3,512,1024]{2,1,0:T(8,128)(2,1)} custom-call(bf16[4,3,128,1024]{3,2,1,0:T(8,128)(2,1)} %bitcast.5), custom_call_target="tpu_custom_call" | custom-call | flops 1000000000 | bytes 9437184 | tf_op jit(solution)/shard_map/exchange/pallas_call | solution.py:114
  278.5 51.4 %reduce-scatter.2.cloned.1.call-done = f32[256,1024]{1,0:T(8,128)} async-done(((f32[4096,1024]{1,0:T(8,128)}), f32[256,1024]{1,0:T(8,128)}) %reduce-scatter.2.cloned.1.call-update) | async-done | bytes 1048592 | tf_op jit(solution)/shard_map/reduce_scatter | solution.py:149
  329.9 2.1 convert_element_type.9
  332.0 1.7 copy.21
  333.7 1.4 copy-done.3
  335.0 1.7 copy.22
  336.7 1.4 copy-done.4
  338.0 1.7 copy.23
  (23 shorter events, 0.6 us)
Async XLA Ops:
  7.2 66.0 %all-gather.5.cloned.1.call-start = ((), (), s32[]{:S(2)}) async-start(), calls=%async_computation.1 | async-start | bytes 10027008 | tf_op jit(solution)/shard_map/all_gather | solution.py:145
  8.5 8.3 %copy-start.5 = (bf16[1024,32]{0,1:T(8,128)(2,1)S(1)}, bf16[1024,32]{0,1:T(8,128)(2,1)}, u32[]{:S(2)}) copy-start(bf16[1024,32]{0,1:T(8,128)(2,1)} %param.12) | copy-start | bytes 196612
  10.5 62.7 %copy-start = (bf16[2,1024,512]{2,1,0:T(8,128)(2,1)S(1)}, bf16[2,1024,512]{2,1,0:T(8,128)(2,1)}, u32[]{:S(2)}) copy-start(bf16[2,1024,512]{2,1,0:T(8,128)(2,1)} %gate_ref.1) | copy-start | bytes 6291460
  10.6 115.9 %all-gather.7.cloned.1.call-start = ((), (), s32[]{:S(2)}) async-start(), calls=%async_computation.3 | async-start | bytes 8912896 | tf_op jit(solution)/shard_map/all_gather | solution.py:157
  12.7 167.0 %all-gather.9.cloned.1.call-start = ((), (), s32[]{:S(2)}) async-start(), calls=%async_computation.4 | async-start | bytes 8912896 | tf_op jit(solution)/shard_map/all_gather | solution.py:157
  14.7 218.1 %all-gather.11.cloned.1.call-start = ((), (), s32[]{:S(2)}) async-start(), calls=%async_computation.5 | async-start | bytes 8912896 | tf_op jit(solution)/shard_map/all_gather | solution.py:157
  16.7 313.2 %reduce-scatter.2.cloned.1.call-start = ((), (), s32[]{:S(2)}) async-start(), calls=%async_computation.2 | async-start | bytes 17825792 | tf_op jit(solution)/shard_map/reduce_scatter | solution.py:149
  73.2 1.6 copy-start.1
  111.0 0.7 copy-start.7
  111.0 1.9 copy-start.6
  241.4 90.5 %copy-start.2 = (bf16[3,1024,512]{2,1,0:T(8,128)(2,1)S(1)}, bf16[3,1024,512]{2,1,0:T(8,128)(2,1)}, u32[]{:S(2)}) copy-start(bf16[3,1024,512]{2,1,0:T(8,128)(2,1)} %exchange.3) | copy-start | bytes 9437188
  332.0 3.0 copy-start.3
  335.0 3.0 copy-start.4
Sparse Core Ops, SparseCore 0:
  10.7 62.4 all-gather.4
  75.4 51.0 all-gather.6
  128.6 51.0 all-gather.8
  181.8 51.0 all-gather.10
  235.0 94.8 reduce-scatter.1

commit v2 on v0

v2 whole, which is shorter than its diff:
```python
import functools

import jax
import jax.numpy as jnp
from jax import lax
from jax.experimental import pallas as pl
from jax.experimental.pallas import tpu as pltpu
from jax.sharding import PartitionSpec as P

ROUTE_SCALE = 2.5
LANES = 128
CORES = 2
MESH = pl.DeviceIdType.MESH


def block_kernel(groups, members, tok_ref, router_ref, table_ref, gate_ref, up_ref, down_ref,
                 y_ref, p_gate_ref, p_up_ref, p_down_ref,
                 toks, gates_all, ups_all, downs_all, piece_gate, piece_up, piece_down,
                 send_gate, send_up, send_down, sums, sums_in, tables, tables_s,
                 load_sem, swap_send, swap_recv, table_send, table_recv,
                 ring_send, ring_recv, sum_send, sum_recv, slot_send, slot_recv, slot_own, ):
    dp = lax.axis_index("dp")
    ep = lax.axis_index("ep")
    chips = members // CORES
    far = chips // 2
    plane = groups * CORES
    z = ep // CORES
    core = lax.rem(ep, CORES)
    q = dp * CORES + core
    above = (dp, lax.rem(z + 1, chips) * CORES + core)
    below = (dp, lax.rem(z + chips - 1, chips) * CORES + core)
    partner = (dp, z * CORES + 1 - core)
    toward = (above, below)
    rows = toks.shape[1]
    half = rows // 2
    width = router_ref.shape[0]
    local = gate_ref.shape[0]
    owned = local * CORES
    slots = p_gate_ref.shape[0]

    def plane_device(k):
        other = lax.rem(q + k, plane)
        return (other // CORES, z * CORES + lax.rem(other, CORES))

    barrier = pltpu.get_barrier_semaphore()
    for device in toward:
        pl.semaphore_signal(barrier, inc=1, device_id=device, device_id_type=MESH)

    def greet(k, _):
        pl.semaphore_signal(barrier, inc=1, device_id=plane_device(k), device_id_type=MESH)
        return 0

    lax.fori_loop(1, plane, greet, 0)
    pl.semaphore_wait(barrier, plane + 1)

    def send(src, dst, send_sem, recv_sem, device):
        copy = pltpu.make_async_remote_copy(src_ref=src, dst_ref=dst, send_sem=send_sem, recv_sem=recv_sem, device_id=device, device_id_type=MESH)
        copy.start()
        return copy

    sent = []

    loads = [pltpu.make_async_copy(tok_ref, toks.at[0], load_sem.at[0])]
    mine = pl.ds(core * local, local)
    swaps = []
    ring = {}
    for d in range(2):
        ring[0, d, 1] = send(tok_ref, toks.at[2 + d], ring_send.at[0, d, 0], ring_recv.at[0, d, 0], toward[d])
    for i, (src, dst) in enumerate(((gate_ref, gates_all), (up_ref, ups_all), (down_ref, downs_all))):
        loads.append(pltpu.make_async_copy(src, dst.at[mine], load_sem.at[1 + i]))
        swaps.append(send(src, dst.at[mine], swap_send.at[i], swap_recv.at[i], partner))
    for load in loads:
        load.start()
    for k in range(1, groups):
        other = lax.rem(dp + k, groups)
        sent.append(send(table_ref, tables.at[dp], table_send.at[k], table_recv.at[k], (other, ep)))
    tables_own = pltpu.make_async_copy(table_ref, tables.at[dp], load_sem.at[4])
    tables_own.start()

    full = (None, gates_all, ups_all, downs_all)
    pieces = (None, piece_gate, piece_up, piece_down)

    def block_of(hop, d, lo=0, count=None):
        origin = lax.rem(z + chips - hop if d == 0 else z + hop, chips)
        return pl.ds(origin * owned + lo, owned if count is None else count)

    def start_piece(i):
        piece = pieces[i].shape[1]
        part = pl.ds(pl.multiple_of(q * piece, piece), piece)
        for d in range(2):
            ring[i, d, 1] = send(full[i].at[:, part, :], pieces[i].at[block_of(0, d)], ring_send.at[i, d, 0], ring_recv.at[i, d, 0], toward[d])
        pieces[i][block_of(0, 0)] = full[i][:, part, :]

    def forward(i, hop):
        for d in range(2):
            ring[i, d, hop - 1].wait_recv()
            if i == 0:
                have, goal = toks.at[2 * (hop - 1) + d], toks.at[2 * hop + d]
                if hop == far:
                    part = pl.ds(d * half, half)
                    have, goal = toks.at[2 * (hop - 1) + d, part], toks.at[1, part]
            else:
                where = block_of(hop - 1, d)
                if hop == far:
                    where = block_of(hop - 1, d, d * (owned // 2), owned // 2)
                have, goal = pieces[i].at[where], pieces[i].at[where]
            ring[i, d, hop] = send(have, goal, ring_send.at[i, d, hop - 1], ring_recv.at[i, d, hop - 1], toward[d])

    def serve(pair):
        both = toks[2 * pair:2 * pair + 2].reshape(2 * rows, toks.shape[2])
        hid = both[:, :width]
        chosen = both[:, width:].astype(jnp.float32) > 0.5
        logits = jnp.dot(hid, router_ref[...], preferred_element_type=jnp.float32)
        gates = jnp.where(chosen, jax.nn.sigmoid(logits), 0.0)
        weights = ROUTE_SCALE * gates / jnp.sum(gates, axis=1, keepdims=True)
        lane = lax.broadcasted_iota(jnp.int32, weights.shape, 1)

        sums[2 * pair:2 * pair + 2] = jnp.zeros((2, rows, width), jnp.float32)

        def expert(e, _):
            hit = (lane == z * owned + e) & chosen
            weight = jnp.sum(jnp.where(hit, weights, 0.0), axis=1, keepdims=True)
            served = jnp.sum(jnp.where(hit, 1.0, 0.0), axis=1, keepdims=True) > 0.5
            act_a = jnp.dot(hid, gates_all[e], preferred_element_type=jnp.float32)
            act_b = jnp.dot(hid, ups_all[e], preferred_element_type=jnp.float32)
            hidden_act = (jax.nn.silu(act_a) * act_b).astype(jnp.bfloat16)
            expert_out = jnp.dot(hidden_act, downs_all[e], preferred_element_type=jnp.float32)
            contrib = jnp.where(served, weight * expert_out.astype(jnp.bfloat16).astype(jnp.float32), 0.0)
            sums[2 * pair:2 * pair + 2] += contrib.reshape(2, rows, width)
            return 0

        lax.fori_loop(0, owned, expert, 0)

    outs = (None, p_gate_ref, p_up_ref, p_down_ref)
    staged = (None, send_gate, send_up, send_down)

    def slot_copy(i, k):
        piece = pieces[i].shape[1]
        place = pl.ds(pl.multiple_of(q * piece, piece), piece)
        return pltpu.make_async_remote_copy(
            src_ref=staged[i].at[k], dst_ref=outs[i].at[:, place, :], send_sem=slot_send.at[i - 1, k], recv_sem=slot_recv.at[i - 1, k],
            device_id=plane_device(k), device_id_type=MESH)

    def slot_copy_own(i):
        piece = pieces[i].shape[1]
        place = pl.ds(pl.multiple_of(q * piece, piece), piece)
        return pltpu.make_async_copy(staged[i].at[0], outs[i].at[:, place, :], slot_own.at[i - 1])

    def exchange(i):
        def pick(k, _):
            group, member = plane_device(k)
            for s in range(slots):
                expert = tables_s[group, 0, member * slots + s]
                staged[i][k, s] = pieces[i][expert]
            return 0

        lax.fori_loop(0, plane, pick, 0)

        def start(k, _):
            slot_copy(i, k).start()
            return 0

        lax.fori_loop(1, plane, start, 0)
        slot_copy_own(i).start()

    def finish(i):
        def wait(k, _):
            slot_copy(i, k).wait()
            return 0

        lax.fori_loop(1, plane, wait, 0)
        slot_copy_own(i).wait()

    def arrived(i, load_index):
        loads[load_index].wait()
        swaps[i - 1].wait()

    arrived(1, 1)
    start_piece(1)
    for hop in range(2, far + 1):
        forward(0, hop)
        forward(1, hop)
        if hop == far:
            arrived(2, 2) if far == 2 else None
            start_piece(2)
            start_piece(3)
        if hop == 2 and far > 2:
            arrived(2, 2)
            arrived(3, 3)
        serve(hop - 1)
    for d in range(2):
        ring[0, d, far].wait_recv()
    loads[0].wait()
    serve(0)
    for copy in sent:
        copy.wait()
    tables_own.wait()
    tables_load = pltpu.make_async_copy(tables, tables_s, load_sem.at[5])
    tables_load.start()
    tables_load.wait()
    for d in range(2):
        ring[1, d, far].wait_recv()
    exchange(1)
    for hop in range(2, far + 1):
        forward(2, hop)
        forward(3, hop)

    sums_sent = []

    def part_of(h):
        return slice(h * half, (h + 1) * half)

    def sum_copy(d, k, h):
        index = 1 if k == far else 2 * k + 1 - d
        copy = send(sums.at[index, pl.ds(h * half, half)], sums_in.at[d, k - 1, pl.ds(h * half, half)],
                    sum_send.at[d, k - 1, h], sum_recv.at[d, k - 1, h], toward[d])
        sums_sent.append(copy)
        return copy

    pending = {}
    for k, h in ((far, 0), (far - 1, 1)):
        for d in range(2):
            pending[d, k, h ^ d] = sum_copy(d, k, h ^ d)
    for i in (2, 3):
        for d in range(2):
            ring[i, d, far].wait_recv()
        exchange(i)
    for k in range(far - 1, 0, -1):
        for h in (0, 1):
            if (k, h) == (far - 1, 1):
                continue
            order = h if k == far - 1 else 1 - h
            for d in range(2):
                part = order ^ d
                pending[d, k + 1, part].wait_recv()
                index = 2 * k + 1 - d
                sums[index, part_of(part)] += sums_in[d, k, part_of(part)]
            for d in range(2):
                pending[d, k, order ^ d] = sum_copy(d, k, order ^ d)
    for h in (1, 0):
        for d in range(2):
            pending[d, 1, h ^ d].wait_recv()
    y_ref[...] = (sums[0] + sums_in[0, 0] + sums_in[1, 0]).astype(jnp.bfloat16)

    for copy in sums_sent:
        copy.wait_send()
    for copy in ring.values():
        copy.wait_send()
    for i in (1, 2, 3):
        finish(i)


def run_block(groups, members, tokens, router, table, w_gate, w_up, w_down, per_dev):
    rows, ext_width = tokens.shape
    local, width, inter = w_gate.shape
    chips = members // CORES
    plane = groups * CORES
    owned = local * CORES
    experts = local * members
    far = chips // 2
    bf16 = w_gate.dtype
    gate_rows, down_rows = width // plane, inter // plane
    dma = pltpu.SemaphoreType.DMA
    anywhere = pl.BlockSpec(memory_space=pl.ANY)
    in_vmem = pl.BlockSpec(memory_space=pltpu.VMEM)
    return pl.pallas_call(
        functools.partial(block_kernel, groups, members),
        out_shape=[
            jax.ShapeDtypeStruct((rows, width), bf16),
            jax.ShapeDtypeStruct((per_dev, width, inter), bf16),
            jax.ShapeDtypeStruct((per_dev, width, inter), bf16),
            jax.ShapeDtypeStruct((per_dev, inter, width), bf16),
        ],
        in_specs=[anywhere, in_vmem, anywhere, anywhere, anywhere, anywhere],
        out_specs=[in_vmem, anywhere, anywhere, anywhere],
        scratch_shapes=[
            pltpu.VMEM((chips, rows, ext_width), bf16),
            pltpu.VMEM((owned, width, inter), bf16),
            pltpu.VMEM((owned, width, inter), bf16),
            pltpu.VMEM((owned, inter, width), bf16),
            pltpu.VMEM((experts, gate_rows, inter), bf16),
            pltpu.VMEM((experts, gate_rows, inter), bf16),
            pltpu.VMEM((experts, down_rows, width), bf16),
            pltpu.VMEM((plane, per_dev, gate_rows, inter), bf16),
            pltpu.VMEM((plane, per_dev, gate_rows, inter), bf16),
            pltpu.VMEM((plane, per_dev, down_rows, width), bf16),
            pltpu.VMEM((chips, rows, width), jnp.float32),
            pltpu.VMEM((2, far, rows, width), jnp.float32),
            pltpu.VMEM((groups, 8, LANES), jnp.int32),
            pltpu.SMEM((groups, 8, LANES), jnp.int32),
            dma((6,)), dma((3,)), dma((3,)), dma((groups,)), dma((groups,)),
            dma((4, 2, far)), dma((4, 2, far)), dma((2, far, 2)), dma((2, far, 2)),
            dma((3, plane)), dma((3, plane)), dma((3,)),
        ],
        compiler_params=pltpu.CompilerParams(collective_id=0, has_side_effects=True, vmem_limit_bytes=67043328),
        name="moe_block",
    )(tokens, router, table, w_gate, w_up, w_down)


def solution(mesh):
    members = mesh.shape["ep"]
    groups = mesh.shape["dp"]
    tok_spec = P(("dp", "ep"), None)
    weight_spec = P("ep", None, None)
    slot_spec = P(("dp", "ep"), None, None)

    def local_block(hid_rows, w_gate, w_up, w_down, w_router, slot_expert, topk_idx, topk_slot):
        width, experts = w_router.shape
        chosen = jnp.any(topk_idx[:, :, None] == jnp.arange(LANES)[None, None, :], axis=1).astype(hid_rows.dtype)
        tokens = jnp.concatenate([hid_rows, chosen], axis=1)
        router = jnp.pad(w_router, ((0, 0), (0, LANES - experts)))
        table = jnp.broadcast_to(jnp.pad(slot_expert, (0, LANES - slot_expert.shape[0]))[None, :], (8, LANES))
        y_rows, p_gate, p_up, p_down = run_block(groups, members, tokens, router, table, w_gate, w_up, w_down, slot_expert.shape[0] // members)
        return y_rows, p_gate, p_up, p_down

    return jax.shard_map(local_block, mesh=mesh, in_specs=(tok_spec, weight_spec, weight_spec, weight_spec, P(None, None), P("dp"), tok_spec, tok_spec), out_specs=(tok_spec, slot_spec, slot_spec, slot_spec), check_vma=False)
```

time: 765 us -> 274 us (0.36)
  waiting for transfers between devices: 307 us -> 0 us
  other arithmetic: 281 us -> 2.36 us
  Pallas kernels: 0 us -> 256 us
  local copies, waits for them, and re-layouts: 96.6 us -> 14.3 us
  blocking collectives: 39.2 us -> 0 us
  matrix products: 21.6 us -> 0 us
  between operations: 14.5 us -> 0.67 us
    scatter-add x2 -> x0, other arithmetic: 261 us -> none  [the longest x1 226 us: serve_pairs(): jax.ops.segment_sum(jnp.ones((num_pairs,), jnp.int32), flat_owner, num_se...]
    pallas_call x0 -> x1, Pallas kernels: none -> 256 us  [run_block(): pl.pallas_call(functools.partial(block_kernel, groups, members), out_shap...]
    all_gather x4 -> x0, waiting for transfers between devices: 209 us -> none  [the longest x1 165 us: local_block(): lax.all_gather(w_gate, 'ep', tiled=True)]
    reduce_scatter x1 -> x0, waiting for transfers between devices: 95 us -> none  [local_block(): y_rows = lax.psum_scatter(partial, 'ep', scatter_dimension=0, tiled=True)]
    gather x14 -> x0, local copies, waits for them, and re-layouts: 81.8 us -> none  [the longest x2 23.9 us: serve_pairs(): rows_in = all_hid[tok_ids]]
    all_gather x2 -> x0, blocking collectives: 39.2 us -> none  [the longest x1 23.4 us: local_block(): all_slot = lax.all_gather(topk_slot, 'ep', tiled=True)]
    dot_general x3 -> x0, matrix products: 21.6 us -> none  [the longest x1 12.7 us: serve_pairs(): jnp.einsum('sci,sih->sch', hidden_act, p_down, preferred_element_type=jnp...]
    unnamed x18 -> x10, local copies, waits for them, and re-layouts: 0.05 us -> 12.3 us
  transfers between devices with their start and end apart: 5 -> 0, of which waited for: 3 -> 0; matrix products, arithmetic and copies ran while one was open for 43% -> 0% of each run, Pallas kernels for 0% -> 0%
where the time goes in v2:
time: 274 us; the launch traced here: 273 us
  Pallas kernels  256 us (93%)
  local copies, waits for them, and re-layouts  14.3 us (5%)
    pallas_call x1, Pallas kernels, run_block(): pl.pallas_call(functools.partial(block_kernel, groups, members), out_shap...  256 us
    unnamed x10, local copies, waits for them, and re-layouts  12.3 us

profile of v2, /device:TPU:21, one launch (start us, length us, event | category | flops | bytes accessed | tf_op | source)
XLA Modules:
  0.0 273.4 jit_solution(15472394288482354617)
XLA Ops:
  0.6 0.7 pad.9
  1.3 0.6 broadcast_in_dim.2.table_ref
  1.9 0.8 copy.13
  2.7 0.4 fusion
  3.2 1.0 copy.14
  4.2 0.8 pad.8.router_ref
  5.0 1.9 pad_maximum_fusion.tok_ref
  6.9 256.0 %moe_block.1 = (bf16[256,1024]{1,0:T(8,128)(2,1)}, bf16[3,1024,512]{2,1,0:T(8,128)(2,1)}, bf16[3,1024,512]{2,1,0:T(8,128)(2,1)}, bf16[3,512,1024]{2,1,0:T(8,128)(2,1)}) custom-call(bf16[256,1152]{1,0:T(8,128)(2,1)} %pad_maximum_fusion.tok_ref, bf16[1024,128]{1,0:T(8,128)(2,1)} %pad.8.router_ref, s32[8,128]{1,0:T(8,128)} %broadcast_in_dim.2.table_ref, ...), custom_call_target="tpu_custom_call" | custom-call | tf_op jit(solution)/shard_map/moe_block/pallas_call | solution.py:266
  262.9 1.9 copy.19
  264.8 0.0 copy-start.1
  264.8 3.9 %copy.20 = bf16[3,1024,512]{2,1,0:T(8,128)(2,1)} copy(bf16[3,1024,512]{2,1,0:T(8,128)(2,1)} %get-tuple-element.9) | data formatting | bytes 6291456
  268.7 0.0 copy-done.1
  268.7 0.0 copy-start
  268.7 1.7 copy.21
  270.4 1.4 copy-done
  271.7 1.7 copy.22
  (1 shorter events, 0.0 us)
Async XLA Ops:
  264.8 3.9 %copy-start.1 = (bf16[3,1024,512]{2,1,0:T(8,128)(2,1)S(1)}, bf16[3,1024,512]{2,1,0:T(8,128)(2,1)}, u32[]{:S(2)}) copy-start(bf16[3,1024,512]{2,1,0:T(8,128)(2,1)} %get-tuple-element.10) | copy-start | bytes 9437188
  268.7 3.0 %copy-start = (bf16[3,512,1024]{2,1,0:T(8,128)(2,1)S(1)}, bf16[3,512,1024]{2,1,0:T(8,128)(2,1)}, u32[]{:S(2)}) copy-start(bf16[3,512,1024]{2,1,0:T(8,128)(2,1)} %get-tuple-element.11) | copy-start | bytes 9437188

commit v3 on v2

v3 whole, which is shorter than its diff:
```python
import functools

import jax
import jax.numpy as jnp
from jax import lax
from jax.experimental import pallas as pl
from jax.experimental.pallas import tpu as pltpu
from jax.sharding import PartitionSpec as P

ROUTE_SCALE = 2.5
LANES = 128
CORES = 2
MESH = pl.DeviceIdType.MESH


def block_kernel(groups, members, tok_ref, idx_ref, router_ref, table_ref, gate_ref, up_ref, down_ref,
                 y_ref, p_gate_ref, p_up_ref, p_down_ref,
                 toks, idxs, gates_all, ups_all, downs_all, piece_gate, piece_up, piece_down,
                 send_gate, send_up, send_down, sums, sums_in, tables, tables_s,
                 load_sem, swap_send, swap_recv, table_send, table_recv, tok_send, tok_recv,
                 ring_send, ring_recv, plane_send, plane_recv, pair_send, pair_recv,
                 sum_send, sum_recv, slot_send, slot_recv, slot_own):
    dp = lax.axis_index("dp")
    ep = lax.axis_index("ep")
    chips = members // CORES
    far = chips // 2
    plane = groups * CORES
    bits = [1 << b for b in range(groups.bit_length() - 1)]
    z = ep // CORES
    core = lax.rem(ep, CORES)
    q = dp * CORES + core
    above = (dp, lax.rem(z + 1, chips) * CORES + core)
    below = (dp, lax.rem(z + chips - 1, chips) * CORES + core)
    partner = (dp, z * CORES + 1 - core)
    toward = (above, below)
    rows, width = toks.shape[1:]
    half = rows // 2
    local = gate_ref.shape[0]
    owned = local * CORES
    slots = p_gate_ref.shape[0]

    def plane_device(k):
        other = lax.rem(q + k, plane)
        return (other // CORES, z * CORES + lax.rem(other, CORES))

    def other_group(r):
        group = dp
        for bit in bits:
            if r & bit:
                group = group + bit * (1 - 2 * lax.rem(dp // bit, 2))
        return group

    barrier = pltpu.get_barrier_semaphore()
    for device in toward:
        pl.semaphore_signal(barrier, inc=1, device_id=device, device_id_type=MESH)

    def greet(k, _):
        pl.semaphore_signal(barrier, inc=1, device_id=plane_device(k), device_id_type=MESH)
        return 0

    lax.fori_loop(1, plane, greet, 0)
    pl.semaphore_wait(barrier, plane + 1)

    sent = []

    def send(src, dst, send_sem, recv_sem, device):
        copy = pltpu.make_async_remote_copy(src_ref=src, dst_ref=dst, send_sem=send_sem, recv_sem=recv_sem, device_id=device, device_id_type=MESH)
        copy.start()
        sent.append(copy)
        return copy

    full = (gates_all, ups_all, downs_all)
    pieces = (piece_gate, piece_up, piece_down)
    staged = (send_gate, send_up, send_down)
    outs = (p_gate_ref, p_up_ref, p_down_ref)
    mine = pl.ds(core * local, local)
    loads = [pltpu.make_async_copy(src, dst.at[mine], load_sem.at[i]) for i, (src, dst) in enumerate(zip((gate_ref, up_ref, down_ref), full))]
    loads.append(pltpu.make_async_copy(tok_ref, toks.at[0], load_sem.at[3]))
    loads.append(pltpu.make_async_copy(idx_ref, idxs.at[0], load_sem.at[4]))
    loads.append(pltpu.make_async_copy(table_ref, tables.at[dp], load_sem.at[5]))
    swaps = []
    ring, toked, planed, paired, summed = {}, {}, {}, {}, {}

    def start():
        for i, src in enumerate((gate_ref, up_ref, down_ref)):
            swaps.append(send(src, full[i].at[mine], swap_send.at[i], swap_recv.at[i], partner))
            loads[i].start()
        for load in loads[3:]:
            load.start()
        for k in range(1, groups):
            swaps.append(send(table_ref, tables.at[dp], table_send.at[k], table_recv.at[k], (lax.rem(dp + k, groups), ep)))

    def arrived(i):
        loads[i].wait()
        swaps[i].wait_recv()
        piece = pieces[i].shape[1]
        pieces[i][block_of(0, 0, 0, owned)] = full[i][:owned, pl.ds(pl.multiple_of(q * piece, piece), piece), :]

    def tokens(hop):
        for d in range(2):
            if hop == 1:
                toked[d, 1, 0] = send(tok_ref, toks.at[2 + d], tok_send.at[d, 0, 0], tok_recv.at[d, 0, 0], toward[d])
                toked[d, 1, 1] = send(idx_ref, idxs.at[2 + d], tok_send.at[d, 0, 1], tok_recv.at[d, 0, 1], toward[d])
            else:
                part = pl.ds(d * half, half)
                toked[d, 2, 0] = send(toks.at[2 + d, part], toks.at[1, part], tok_send.at[d, 1, 0], tok_recv.at[d, 1, 0], toward[d])
                toked[d, 2, 1] = send(idxs.at[2 + d, :, part], idxs.at[1, :, part], tok_send.at[d, 1, 1], tok_recv.at[d, 1, 1], toward[d])

    def tokens_near():
        for d in range(2):
            for a in range(2):
                toked[d, 1, a].wait_recv()

    def tokens_far():
        loads[3].wait()
        loads[4].wait()
        for d in range(2):
            for a in range(2):
                toked[d, 2, a].wait_recv()

    def block_of(hop, d, lo, count):
        origin = lax.rem(z + chips - hop if d == 0 else z + hop, chips)
        return pl.ds(origin * owned + lo, count)

    def pass_on(i, short, hop):
        piece = pieces[i].shape[1]
        for d in range(2):
            h = 1 - d if short else d
            where = block_of(hop - 1, d, h * local, local)
            src = pieces[i].at[where]
            if hop == 1:
                src = full[i].at[pl.ds(h * local, local), pl.ds(pl.multiple_of(q * piece, piece), piece), :]
            else:
                ring[i, d, h, hop - 1].wait_recv()
            ring[i, d, h, hop] = send(src, pieces[i].at[where], ring_send.at[i, d, h, hop - 1], ring_recv.at[i, d, h, hop - 1], toward[d])

    def rebuild(i, step):
        piece = pieces[i].shape[1]

        def region(h, r):
            at = (other_group(r) * CORES + core) * piece
            return (pl.ds(owned + h * local, local), pl.ds(pl.multiple_of(at, piece), piece), slice(None))

        for h in range(2):
            own = block_of(far, h, h * local, local)
            ways = bits if h == 0 else bits[::-1]
            seen, fresh = [0], [0]
            for bit in ways[:step]:
                fresh = [r | bit for r in seen]
                seen = seen + fresh
            if step == 0:
                ring[i, h, h, far].wait_recv()
                full[i][region(h, 0)] = pieces[i][own]
            for r in fresh:
                if r:
                    planed[i, h, r].wait_recv()
                src = full[i].at[region(h, r)] if r else pieces[i].at[own]
                paired[i, h, r] = send(src, full[i].at[region(h, r)], pair_send.at[i, h, r], pair_recv.at[i, h, r], partner)
            if step < len(ways):
                bit = ways[step]
                for r in seen:
                    src = full[i].at[region(h, r)] if r else pieces[i].at[own]
                    planed[i, h, r | bit] = send(src, full[i].at[region(h, r)], plane_send.at[i, h, r | bit], plane_recv.at[i, h, r | bit], (other_group(bit), ep))

    def rebuilt():
        for copy in paired.values():
            copy.wait_recv()

    def serve(pair, second):
        hid = toks[2 * pair:2 * pair + 2].reshape(2 * rows, width)
        idx = jnp.concatenate([idxs[2 * pair], idxs[2 * pair + 1]], axis=1)
        router = router_ref[...]
        logits = lax.dot_general(router, hid, (((1,), (1,)), ((), ())), preferred_element_type=jnp.float32)
        name = lax.broadcasted_iota(jnp.int32, logits.shape, 0)
        chosen = name == idx[0:1]
        for j in range(1, idx.shape[0]):
            chosen = chosen | (name == idx[j:j + 1])
        gates = jnp.where(chosen, jax.nn.sigmoid(logits), 0.0)
        weights = ROUTE_SCALE * gates / jnp.sum(gates, axis=0, keepdims=True)
        weights = jnp.where(chosen, weights, -1.0)
        weights = jnp.concatenate([weights, jnp.full((LANES - weights.shape[0], weights.shape[1]), -1.0, jnp.float32)], axis=0).T
        lane = lax.broadcasted_iota(jnp.int32, weights.shape, 1)
        first = lax.rem(z + far * second, chips) * owned
        if not second:
            sums[2 * pair:2 * pair + 2] = jnp.zeros((2, rows, width), jnp.float32)

        def expert(e, _):
            weight = jnp.sum(jnp.where(lane == first + e, weights, 0.0), axis=1, keepdims=True)
            at = e + owned * second
            act_a = jnp.dot(hid, gates_all[at], preferred_element_type=jnp.float32)
            act_b = jnp.dot(hid, ups_all[at], preferred_element_type=jnp.float32)
            hidden_act = (jax.nn.silu(act_a) * act_b).astype(jnp.bfloat16)
            expert_out = jnp.dot(hidden_act, downs_all[at], preferred_element_type=jnp.float32)
            contrib = jnp.where(weight < 0.0, 0.0, weight * expert_out.astype(jnp.bfloat16).astype(jnp.float32))
            sums[2 * pair:2 * pair + 2] += contrib.reshape(2, rows, width)
            return 0

        lax.fori_loop(0, owned, expert, 0)

    def slot_copy(i, k):
        piece = pieces[i].shape[1]
        place = pl.ds(pl.multiple_of(q * piece, piece), piece)
        return pltpu.make_async_remote_copy(
            src_ref=staged[i].at[k], dst_ref=outs[i].at[:, place, :], send_sem=slot_send.at[i, k], recv_sem=slot_recv.at[i, k],
            device_id=plane_device(k), device_id_type=MESH)

    def slot_copy_own(i):
        piece = pieces[i].shape[1]
        place = pl.ds(pl.multiple_of(q * piece, piece), piece)
        return pltpu.make_async_copy(staged[i].at[0], outs[i].at[:, place, :], slot_own.at[i])

    def tables_ready():
        loads[5].wait()
        for copy in swaps[3:]:
            copy.wait_recv()
        load = pltpu.make_async_copy(tables, tables_s, load_sem.at[6])
        load.start()
        load.wait()

    def exchange(i):
        for d in range(2):
            ring[i, d, 1 - d, far - 1].wait_recv()

        def pick(k, _):
            group, member = plane_device(k)
            for s in range(slots):
                staged[i][k, s] = pieces[i][tables_s[group, 0, member * slots + s]]
            return 0

        def begin(k, _):
            slot_copy(i, k).start()
            return 0

        lax.fori_loop(0, plane, pick, 0)
        lax.fori_loop(1, plane, begin, 0)
        slot_copy_own(i).start()

    def finish(i):
        def wait(k, _):
            slot_copy(i, k).wait()
            return 0

        lax.fori_loop(1, plane, wait, 0)
        slot_copy_own(i).wait()

    def part_of(h):
        return slice(h * half, (h + 1) * half)

    def sum_copy(d, k, h):
        index = 1 if k == 2 else 3 - d
        part = pl.ds(h * half, half)
        summed[d, k, h] = send(sums.at[index, part], sums_in.at[d, k - 1, part], sum_send.at[d, k - 1, h], sum_recv.at[d, k - 1, h], toward[d])

    def sums_far():
        for d in range(2):
            sum_copy(d, 2, 1 - d)

    def sums_near():
        for d in range(2):
            sum_copy(d, 1, d)

    def sums_joined():
        for d in range(2):
            summed[d, 2, 1 - d].wait_recv()
            sums[3 - d, part_of(1 - d)] += sums_in[d, 1, part_of(1 - d)]
        for d in range(2):
            sum_copy(d, 1, 1 - d)

    gate, up, down, long, short = 0, 1, 2, 0, 1
    last = len(bits)
    start()
    tokens(1)
    arrived(gate)
    pass_on(gate, long, 1)
    pass_on(gate, short, 1)
    pass_on(gate, long, 2)
    pass_on(gate, long, 3)
    pass_on(gate, short, 2)
    pass_on(gate, long, 4)
    pass_on(gate, short, 3)
    arrived(up)
    pass_on(up, long, 1)
    rebuild(gate, 0)
    arrived(down)
    pass_on(down, long, 1)
    tables_ready()
    exchange(gate)
    pass_on(up, long, 2)
    pass_on(down, long, 2)
    pass_on(up, long, 3)
    rebuild(gate, 1)
    pass_on(down, long, 3)
    pass_on(up, long, 4)
    pass_on(down, long, 4)
    rebuild(up, 0)
    pass_on(up, short, 1)
    tokens_near()
    serve(1, 0)
    rebuild(down, 0)
    tokens(2)
    rebuild(up, 1)
    pass_on(up, short, 2)
    rebuild(down, 1)
    pass_on(up, short, 3)
    pass_on(down, short, 1)
    for step in range(2, last + 1):
        rebuild(gate, step)
    exchange(up)
    pass_on(down, short, 2)
    pass_on(down, short, 3)
    for step in range(2, last + 1):
        rebuild(up, step)
    tokens_far()
    serve(0, 0)
    for step in range(2, last + 1):
        rebuild(down, step)
    rebuilt()
    serve(0, 1)
    sums_far()
    exchange(down)
    serve(1, 1)
    sums_near()
    sums_joined()
    for d in range(2):
        for h in range(2):
            summed[d, 1, h].wait_recv()
    y_ref[...] = (sums[0] + sums_in[0, 0] + sums_in[1, 0]).astype(jnp.bfloat16)
    for copy in sent:
        copy.wait_send()
    for i in range(3):
        finish(i)


def run_block(groups, members, tokens, idx, router, table, w_gate, w_up, w_down, per_dev):
    rows, width = tokens.shape
    local, _, inter = w_gate.shape
    chips = members // CORES
    far = chips // 2
    plane = groups * CORES
    owned = local * CORES
    experts = local * members
    bf16 = w_gate.dtype
    gate_rows, down_rows = width // plane, inter // plane
    dma = pltpu.SemaphoreType.DMA
    anywhere = pl.BlockSpec(memory_space=pl.ANY)
    in_vmem = pl.BlockSpec(memory_space=pltpu.VMEM)
    return pl.pallas_call(
        functools.partial(block_kernel, groups, members),
        out_shape=[
            jax.ShapeDtypeStruct((rows, width), bf16),
            jax.ShapeDtypeStruct((per_dev, width, inter), bf16),
            jax.ShapeDtypeStruct((per_dev, width, inter), bf16),
            jax.ShapeDtypeStruct((per_dev, inter, width), bf16),
        ],
        in_specs=[anywhere, anywhere, in_vmem, anywhere, anywhere, anywhere, anywhere],
        out_specs=[in_vmem, anywhere, anywhere, anywhere],
        scratch_shapes=[
            pltpu.VMEM((4, rows, width), bf16),
            pltpu.VMEM((4,) + idx.shape, jnp.int32),
            pltpu.VMEM((2 * owned, width, inter), bf16),
            pltpu.VMEM((2 * owned, width, inter), bf16),
            pltpu.VMEM((2 * owned, inter, width), bf16),
            pltpu.VMEM((experts, gate_rows, inter), bf16),
            pltpu.VMEM((experts, gate_rows, inter), bf16),
            pltpu.VMEM((experts, down_rows, width), bf16),
            pltpu.VMEM((plane, per_dev, gate_rows, inter), bf16),
            pltpu.VMEM((plane, per_dev, gate_rows, inter), bf16),
            pltpu.VMEM((plane, per_dev, down_rows, width), bf16),
            pltpu.VMEM((4, rows, width), jnp.float32),
            pltpu.VMEM((2, 2, rows, width), jnp.float32),
            pltpu.VMEM((groups, 8, LANES), jnp.int32),
            pltpu.SMEM((groups, 8, LANES), jnp.int32),
            dma((7,)), dma((3,)), dma((3,)), dma((groups,)), dma((groups,)), dma((2, 2, 2)), dma((2, 2, 2)),
            dma((3, 2, 2, far)), dma((3, 2, 2, far)), dma((3, 2, groups)), dma((3, 2, groups)), dma((3, 2, groups)), dma((3, 2, groups)),
            dma((2, 2, 2)), dma((2, 2, 2)), dma((3, plane)), dma((3, plane)), dma((3,)),
        ],
        compiler_params=pltpu.CompilerParams(collective_id=0, has_side_effects=True, vmem_limit_bytes=67043328),
        name="moe_block",
    )(tokens, idx, router, table, w_gate, w_up, w_down)


def solution(mesh):
    members = mesh.shape["ep"]
    groups = mesh.shape["dp"]
    tok_spec = P(("dp", "ep"), None)
    weight_spec = P("ep", None, None)
    slot_spec = P(("dp", "ep"), None, None)

    def local_block(hid_rows, w_gate, w_up, w_down, w_router, slot_expert, topk_idx, topk_slot):
        table = jnp.broadcast_to(jnp.pad(slot_expert, (0, LANES - slot_expert.shape[0]))[None, :], (8, LANES))
        y_rows, p_gate, p_up, p_down = run_block(groups, members, hid_rows, topk_idx.T, w_router.T, table, w_gate, w_up, w_down, slot_expert.shape[0] // members)
        return y_rows, p_gate, p_up, p_down

    return jax.shard_map(local_block, mesh=mesh, in_specs=(tok_spec, weight_spec, weight_spec, weight_spec, P(None, None), P("dp"), tok_spec, tok_spec), out_specs=(tok_spec, slot_spec, slot_spec, slot_spec), check_vma=False)
```

time: 274 us -> 227 us (0.83)
  Pallas kernels: 256 us -> 215 us
    pallas_call x1, Pallas kernels: 256 us -> 215 us  [run_block(): pl.pallas_call(functools.partial(block_kernel, groups, members), out_shap...]
    unnamed x10 -> x8, local copies, waits for them, and re-layouts: 12.3 us -> 10.5 us
where the time goes in v3:
time: 227 us
  Pallas kernels  215 us (95%)
  local copies, waits for them, and re-layouts  11.7 us (5%)
    pallas_call x1, Pallas kernels, run_block(): pl.pallas_call(functools.partial(block_kernel, groups, members), out_shap...  215 us
    unnamed x8, local copies, waits for them, and re-layouts  10.5 us

profile of v3, /device:TPU:21, one launch (start us, length us, event | category | flops | bytes accessed | tf_op | source)
XLA Modules:
  0.0 227.0 jit_solution(708770669831018898)
XLA Ops:
  0.6 0.7 pad.4
  1.3 0.6 broadcast_in_dim.2.table_ref
  1.9 214.6 %moe_block.1 = (bf16[256,1024]{1,0:T(8,128)(2,1)}, bf16[3,1024,512]{2,1,0:T(8,128)(2,1)}, bf16[3,1024,512]{2,1,0:T(8,128)(2,1)}, bf16[3,512,1024]{2,1,0:T(8,128)(2,1)}) custom-call(bf16[256,1024]{1,0:T(8,128)(2,1)} %tok_ref.1, s32[8,256]{1,0:T(8,128)} %bitcast.3, bf16[32,1024]{1,0:T(8,128)(2,1)} %bitcast.2, s32[8,128]{1,0:T(8,128)} %broadcast_in_dim.2.table_ref, ...), custom_call_target="tpu_custom_call" | custom-call | tf_op jit(solution)/shard_map/moe_block/pallas_call | solution.py:347
  216.5 1.9 copy.15
  218.4 0.0 copy-start.1
  218.4 3.9 %copy.16 = bf16[3,1024,512]{2,1,0:T(8,128)(2,1)} copy(bf16[3,1024,512]{2,1,0:T(8,128)(2,1)} %get-tuple-element.9) | data formatting | bytes 6291456
  222.3 0.0 copy-done.1
  222.3 0.0 copy-start
  222.3 1.7 copy.17
  224.0 1.4 copy-done
  225.3 1.7 copy.18
Async XLA Ops:
  218.4 3.9 %copy-start.1 = (bf16[3,1024,512]{2,1,0:T(8,128)(2,1)S(1)}, bf16[3,1024,512]{2,1,0:T(8,128)(2,1)}, u32[]{:S(2)}) copy-start(bf16[3,1024,512]{2,1,0:T(8,128)(2,1)} %get-tuple-element.10) | copy-start | bytes 9437188
  222.3 3.0 %copy-start = (bf16[3,512,1024]{2,1,0:T(8,128)(2,1)S(1)}, bf16[3,512,1024]{2,1,0:T(8,128)(2,1)}, u32[]{:S(2)}) copy-start(bf16[3,512,1024]{2,1,0:T(8,128)(2,1)} %get-tuple-element.11) | copy-start | bytes 9437188

commit v4 on v3

--- a/solution.py
+++ b/solution.py
@@ -17,7 +17,7 @@
                  y_ref, p_gate_ref, p_up_ref, p_down_ref,
                  toks, idxs, gates_all, ups_all, downs_all, piece_gate, piece_up, piece_down,
                  send_gate, send_up, send_down, sums, sums_in, tables, tables_s,
-                 load_sem, swap_send, swap_recv, table_send, table_recv, tok_send, tok_recv,
+                 load_sem, own_sem, early_send, early_recv, swap_send, swap_recv, table_send, table_recv, tok_send, tok_recv,
                  ring_send, ring_recv, plane_send, plane_recv, pair_send, pair_recv,
                  sum_send, sum_recv, slot_send, slot_recv, slot_own):
     dp = lax.axis_index("dp")
@@ -79,9 +79,17 @@
     loads.append(pltpu.make_async_copy(idx_ref, idxs.at[0], load_sem.at[4]))
     loads.append(pltpu.make_async_copy(table_ref, tables.at[dp], load_sem.at[5]))
     swaps = []
+    owns, earlies = [], []
     ring, toked, planed, paired, summed = {}, {}, {}, {}, {}
 
     def start():
+        for i, src in enumerate((gate_ref, up_ref, down_ref)):
+            piece = pieces[i].shape[1]
+            place = pieces[i].at[block_of(0, 0, core * local, local)]
+            theirs = (q + 1 - 2 * core) * piece
+            earlies.append(send(src.at[:, pl.ds(pl.multiple_of(theirs, piece), piece), :], place, early_send.at[i], early_recv.at[i], partner))
+            owns.append(pltpu.make_async_copy(src.at[:, pl.ds(pl.multiple_of(q * piece, piece), piece), :], place, own_sem.at[i]))
+            owns[i].start()
         for i, src in enumerate((gate_ref, up_ref, down_ref)):
             swaps.append(send(src, full[i].at[mine], swap_send.at[i], swap_recv.at[i], partner))
             loads[i].start()
@@ -91,10 +99,13 @@
             swaps.append(send(table_ref, tables.at[dp], table_send.at[k], table_recv.at[k], (lax.rem(dp + k, groups), ep)))
 
     def arrived(i):
-        loads[i].wait()
-        swaps[i].wait_recv()
-        piece = pieces[i].shape[1]
-        pieces[i][block_of(0, 0, 0, owned)] = full[i][:owned, pl.ds(pl.multiple_of(q * piece, piece), piece), :]
+        owns[i].wait()
+        earlies[i].wait_recv()
+
+    def experts_ready():
+        for i in range(3):
+            loads[i].wait()
+            swaps[i].wait_recv()
 
     def tokens(hop):
         for d in range(2):
@@ -122,45 +133,41 @@
         origin = lax.rem(z + chips - hop if d == 0 else z + hop, chips)
         return pl.ds(origin * owned + lo, count)
 
-    def pass_on(i, short, hop):
-        piece = pieces[i].shape[1]
+    def pass_on(i, short, hop, e):
         for d in range(2):
             h = 1 - d if short else d
-            where = block_of(hop - 1, d, h * local, local)
-            src = pieces[i].at[where]
-            if hop == 1:
-                src = full[i].at[pl.ds(h * local, local), pl.ds(pl.multiple_of(q * piece, piece), piece), :]
-            else:
-                ring[i, d, h, hop - 1].wait_recv()
-            ring[i, d, h, hop] = send(src, pieces[i].at[where], ring_send.at[i, d, h, hop - 1], ring_recv.at[i, d, h, hop - 1], toward[d])
-
-    def rebuild(i, step):
+            where = pieces[i].at[block_of(hop - 1, d, h * local + e, 1)]
+            if hop > 1:
+                ring[i, d, h, e, hop - 1].wait_recv()
+            ring[i, d, h, e, hop] = send(where, where, ring_send.at[i, d, h, e, hop - 1], ring_recv.at[i, d, h, e, hop - 1], toward[d])
+
+    def rebuild(i, step, e):
         piece = pieces[i].shape[1]
 
         def region(h, r):
             at = (other_group(r) * CORES + core) * piece
-            return (pl.ds(owned + h * local, local), pl.ds(pl.multiple_of(at, piece), piece), slice(None))
+            return (pl.ds(owned + h * local + e, 1), pl.ds(pl.multiple_of(at, piece), piece), slice(None))
 
         for h in range(2):
-            own = block_of(far, h, h * local, local)
+            own = block_of(far, h, h * local + e, 1)
             ways = bits if h == 0 else bits[::-1]
             seen, fresh = [0], [0]
             for bit in ways[:step]:
                 fresh = [r | bit for r in seen]
                 seen = seen + fresh
             if step == 0:
-                ring[i, h, h, far].wait_recv()
+                ring[i, h, h, e, far].wait_recv()
                 full[i][region(h, 0)] = pieces[i][own]
             for r in fresh:
                 if r:
-                    planed[i, h, r].wait_recv()
+                    planed[i, h, e, r].wait_recv()
                 src = full[i].at[region(h, r)] if r else pieces[i].at[own]
-                paired[i, h, r] = send(src, full[i].at[region(h, r)], pair_send.at[i, h, r], pair_recv.at[i, h, r], partner)
+                paired[i, h, e, r] = send(src, full[i].at[region(h, r)], pair_send.at[i, h, e, r], pair_recv.at[i, h, e, r], partner)
             if step < len(ways):
                 bit = ways[step]
                 for r in seen:
                     src = full[i].at[region(h, r)] if r else pieces[i].at[own]
-                    planed[i, h, r | bit] = send(src, full[i].at[region(h, r)], plane_send.at[i, h, r | bit], plane_recv.at[i, h, r | bit], (other_group(bit), ep))
+                    planed[i, h, e, r | bit] = send(src, full[i].at[region(h, r)], plane_send.at[i, h, e, r | bit], plane_recv.at[i, h, e, r | bit], (other_group(bit), ep))
 
     def rebuilt():
         for copy in paired.values():
@@ -219,7 +226,8 @@
 
     def exchange(i):
         for d in range(2):
-            ring[i, d, 1 - d, far - 1].wait_recv()
+            for e in range(local):
+                ring[i, d, 1 - d, e, far - 1].wait_recv()
 
         def pick(k, _):
             group, member = plane_device(k)
@@ -269,51 +277,85 @@
     gate, up, down, long, short = 0, 1, 2, 0, 1
     last = len(bits)
     start()
-    tokens(1)
     arrived(gate)
-    pass_on(gate, long, 1)
-    pass_on(gate, short, 1)
-    pass_on(gate, long, 2)
-    pass_on(gate, long, 3)
-    pass_on(gate, short, 2)
-    pass_on(gate, long, 4)
-    pass_on(gate, short, 3)
+    pass_on(gate, long, 1, 0)
+    pass_on(gate, long, 1, 1)
+    pass_on(gate, long, 2, 0)
+    pass_on(gate, long, 2, 1)
+    pass_on(gate, short, 1, 0)
+    pass_on(gate, long, 3, 1)
+    pass_on(gate, long, 3, 0)
+    pass_on(gate, short, 1, 1)
+    pass_on(gate, long, 4, 1)
+    pass_on(gate, long, 4, 0)
+    pass_on(gate, short, 2, 1)
+    rebuild(gate, 0, 1)
+    pass_on(gate, short, 2, 0)
+    rebuild(gate, 0, 0)
+    pass_on(gate, short, 3, 1)
+    rebuild(gate, 1, 1)
+    pass_on(gate, short, 3, 0)
+    rebuild(gate, 1, 0)
+    arrived(down)
+    pass_on(down, long, 1, 1)
+    pass_on(down, long, 1, 0)
     arrived(up)
-    pass_on(up, long, 1)
-    rebuild(gate, 0)
-    arrived(down)
-    pass_on(down, long, 1)
+    pass_on(up, long, 1, 1)
     tables_ready()
     exchange(gate)
-    pass_on(up, long, 2)
-    pass_on(down, long, 2)
-    pass_on(up, long, 3)
-    rebuild(gate, 1)
-    pass_on(down, long, 3)
-    pass_on(up, long, 4)
-    pass_on(down, long, 4)
-    rebuild(up, 0)
-    pass_on(up, short, 1)
+    pass_on(down, long, 2, 1)
+    pass_on(up, long, 1, 0)
+    pass_on(up, long, 2, 1)
+    pass_on(up, long, 2, 0)
+    pass_on(up, long, 3, 1)
+    pass_on(up, long, 3, 0)
+    pass_on(up, long, 4, 1)
+    for step in range(2, last + 1):
+        rebuild(gate, step, 1)
+    pass_on(down, long, 2, 0)
+    pass_on(up, long, 4, 0)
+    pass_on(down, long, 3, 1)
+    pass_on(down, long, 3, 0)
+    rebuild(up, 0, 1)
+    for step in range(2, last + 1):
+        rebuild(gate, step, 0)
+    rebuild(up, 0, 0)
+    pass_on(up, short, 1, 0)
+    pass_on(up, short, 1, 1)
+    pass_on(down, long, 4, 0)
+    rebuild(up, 1, 1)
+    pass_on(up, short, 2, 0)
+    pass_on(down, long, 4, 1)
+    rebuild(down, 0, 0)
+    pass_on(up, short, 2, 1)
+    pass_on(up, short, 3, 0)
+    rebuild(up, 1, 0)
+    pass_on(up, short, 3, 1)
+    rebuild(down, 0, 1)
+    tokens(1)
+    rebuild(down, 1, 0)
+    rebuild(down, 1, 1)
+    pass_on(down, short, 1, 1)
+    for step in range(2, last + 1):
+        rebuild(up, step, 0)
+    exchange(up)
+    for step in range(2, last + 1):
+        rebuild(down, step, 0)
+    pass_on(down, short, 1, 0)
     tokens_near()
+    tokens(2)
+    experts_ready()
     serve(1, 0)
-    rebuild(down, 0)
-    tokens(2)
-    rebuild(up, 1)
-    pass_on(up, short, 2)
-    rebuild(down, 1)
-    pass_on(up, short, 3)
-    pass_on(down, short, 1)
-    for step in range(2, last + 1):
-        rebuild(gate, step)
-    exchange(up)
-    pass_on(down, short, 2)
-    pass_on(down, short, 3)
-    for step in range(2, last + 1):
-        rebuild(up, step)
+    pass_on(down, short, 2, 0)
+    for step in range(2, last + 1):
+        rebuild(up, step, 1)
+    for step in range(2, last + 1):
+        rebuild(down, step, 1)
+    pass_on(down, short, 2, 1)
     tokens_far()
     serve(0, 0)
-    for step in range(2, last + 1):
-        rebuild(down, step)
+    pass_on(down, short, 3, 0)
+    pass_on(down, short, 3, 1)
     rebuilt()
     serve(0, 1)
     sums_far()
@@ -370,8 +412,9 @@
             pltpu.VMEM((2, 2, rows, width), jnp.float32),
             pltpu.VMEM((groups, 8, LANES), jnp.int32),
             pltpu.SMEM((groups, 8, LANES), jnp.int32),
-            dma((7,)), dma((3,)), dma((3,)), dma((groups,)), dma((groups,)), dma((2, 2, 2)), dma((2, 2, 2)),
-            dma((3, 2, 2, far)), dma((3, 2, 2, far)), dma((3, 2, groups)), dma((3, 2, groups)), dma((3, 2, groups)), dma((3, 2, groups)),
+            dma((7,)), dma((3,)), dma((3,)), dma((3,)), dma((3,)), dma((3,)), dma((groups,)), dma((groups,)), dma((2, 2, 2)), dma((2, 2, 2)),
+            dma((3, 2, 2, local, far)), dma((3, 2, 2, local, far)),
+            dma((3, 2, local, groups)), dma((3, 2, local, groups)), dma((3, 2, local, groups)), dma((3, 2, local, groups)),
             dma((2, 2, 2)), dma((2, 2, 2)), dma((3, plane)), dma((3, plane)), dma((3,)),
         ],
         compiler_params=pltpu.CompilerParams(collective_id=0, has_side_effects=True, vmem_limit_bytes=67043328),

time: 227 us -> 210 us (0.925)
  Pallas kernels: 215 us -> 198 us
    pallas_call x1, Pallas kernels: 215 us -> 198 us  [run_block(): pl.pallas_call(functools.partial(block_kernel, groups, members), out_shap...]
where the time goes in v4:
time: 210 us
  Pallas kernels  198 us (94%)
  local copies, waits for them, and re-layouts  11.7 us (6%)
    pallas_call x1, Pallas kernels, run_block(): pl.pallas_call(functools.partial(block_kernel, groups, members), out_shap...  198 us
    unnamed x8, local copies, waits for them, and re-layouts  10.5 us

profile of v4, /device:TPU:21, one launch (start us, length us, event | category | flops | bytes accessed | tf_op | source)
XLA Modules:
  0.0 209.9 jit_solution(11578857781670235718)
XLA Ops:
  0.6 0.7 pad.4
  1.3 0.6 broadcast_in_dim.2.table_ref
  1.9 197.6 %moe_block.1 = (bf16[256,1024]{1,0:T(8,128)(2,1)}, bf16[3,1024,512]{2,1,0:T(8,128)(2,1)}, bf16[3,1024,512]{2,1,0:T(8,128)(2,1)}, bf16[3,512,1024]{2,1,0:T(8,128)(2,1)}) custom-call(bf16[256,1024]{1,0:T(8,128)(2,1)} %tok_ref.1, s32[8,256]{1,0:T(8,128)} %bitcast.3, bf16[32,1024]{1,0:T(8,128)(2,1)} %bitcast.2, s32[8,128]{1,0:T(8,128)} %broadcast_in_dim.2.table_ref, ...), custom_call_target="tpu_custom_call" | custom-call | tf_op jit(solution)/shard_map/moe_block/pallas_call | solution.py:389
  199.5 1.9 copy.15
  201.3 0.0 copy-start.1
  201.3 3.9 %copy.16 = bf16[3,1024,512]{2,1,0:T(8,128)(2,1)} copy(bf16[3,1024,512]{2,1,0:T(8,128)(2,1)} %get-tuple-element.9) | data formatting | bytes 6291456
  205.2 0.0 copy-done.1
  205.2 0.0 copy-start
  205.2 1.7 copy.17
  206.9 1.4 copy-done
  208.3 1.7 copy.18
Async XLA Ops:
  201.3 3.9 %copy-start.1 = (bf16[3,1024,512]{2,1,0:T(8,128)(2,1)S(1)}, bf16[3,1024,512]{2,1,0:T(8,128)(2,1)}, u32[]{:S(2)}) copy-start(bf16[3,1024,512]{2,1,0:T(8,128)(2,1)} %get-tuple-element.10) | copy-start | bytes 9437188
  205.2 3.0 %copy-start = (bf16[3,512,1024]{2,1,0:T(8,128)(2,1)S(1)}, bf16[3,512,1024]{2,1,0:T(8,128)(2,1)}, u32[]{:S(2)}) copy-start(bf16[3,512,1024]{2,1,0:T(8,128)(2,1)} %get-tuple-element.11) | copy-start | bytes 9437188

commit v5 on v4

--- a/solution.py
+++ b/solution.py
@@ -16,7 +16,7 @@
 def block_kernel(groups, members, tok_ref, idx_ref, router_ref, table_ref, gate_ref, up_ref, down_ref,
                  y_ref, p_gate_ref, p_up_ref, p_down_ref,
                  toks, idxs, gates_all, ups_all, downs_all, piece_gate, piece_up, piece_down,
-                 send_gate, send_up, send_down, sums, sums_in, tables, tables_s,
+                 send_gate, send_down, sums, sums_in, sums_mid, tables, tables_s,
                  load_sem, own_sem, early_send, early_recv, swap_send, swap_recv, table_send, table_recv, tok_send, tok_recv,
                  ring_send, ring_recv, plane_send, plane_recv, pair_send, pair_recv,
                  sum_send, sum_recv, slot_send, slot_recv, slot_own):
@@ -71,7 +71,7 @@
 
     full = (gates_all, ups_all, downs_all)
     pieces = (piece_gate, piece_up, piece_down)
-    staged = (send_gate, send_up, send_down)
+    staged = (send_gate, send_gate, send_down)
     outs = (p_gate_ref, p_up_ref, p_down_ref)
     mine = pl.ds(core * local, local)
     loads = [pltpu.make_async_copy(src, dst.at[mine], load_sem.at[i]) for i, (src, dst) in enumerate(zip((gate_ref, up_ref, down_ref), full))]
@@ -239,17 +239,26 @@
             slot_copy(i, k).start()
             return 0
 
+        if i == 1:
+            left(0)
         lax.fori_loop(0, plane, pick, 0)
         lax.fori_loop(1, plane, begin, 0)
         slot_copy_own(i).start()
 
-    def finish(i):
+    def left(i):
         def wait(k, _):
-            slot_copy(i, k).wait()
+            slot_copy(i, k).wait_send()
             return 0
 
         lax.fori_loop(1, plane, wait, 0)
         slot_copy_own(i).wait()
+
+    def landed(i):
+        def wait(k, _):
+            slot_copy(i, k).wait_recv()
+            return 0
+
+        lax.fori_loop(1, plane, wait, 0)
 
     def part_of(h):
         return slice(h * half, (h + 1) * half)
@@ -257,7 +266,7 @@
     def sum_copy(d, k, h):
         index = 1 if k == 2 else 3 - d
         part = pl.ds(h * half, half)
-        summed[d, k, h] = send(sums.at[index, part], sums_in.at[d, k - 1, part], sum_send.at[d, k - 1, h], sum_recv.at[d, k - 1, h], toward[d])
+        summed[d, k, h] = send(sums.at[index, part], sums_mid.at[d] if k == 2 else sums_in.at[d, part], sum_send.at[d, k - 1, h], sum_recv.at[d, k - 1, h], toward[d])
 
     def sums_far():
         for d in range(2):
@@ -270,7 +279,7 @@
     def sums_joined():
         for d in range(2):
             summed[d, 2, 1 - d].wait_recv()
-            sums[3 - d, part_of(1 - d)] += sums_in[d, 1, part_of(1 - d)]
+            sums[3 - d, part_of(1 - d)] += sums_mid[d]
         for d in range(2):
             sum_copy(d, 1, 1 - d)
 
@@ -366,11 +375,13 @@
     for d in range(2):
         for h in range(2):
             summed[d, 1, h].wait_recv()
-    y_ref[...] = (sums[0] + sums_in[0, 0] + sums_in[1, 0]).astype(jnp.bfloat16)
+    y_ref[...] = (sums[0] + sums_in[0] + sums_in[1]).astype(jnp.bfloat16)
     for copy in sent:
         copy.wait_send()
+    left(1)
+    left(2)
     for i in range(3):
-        finish(i)
+        landed(i)
 
 
 def run_block(groups, members, tokens, idx, router, table, w_gate, w_up, w_down, per_dev):
@@ -389,13 +400,13 @@
     return pl.pallas_call(
         functools.partial(block_kernel, groups, members),
         out_shape=[
-            jax.ShapeDtypeStruct((rows, width), bf16),
-            jax.ShapeDtypeStruct((per_dev, width, inter), bf16),
-            jax.ShapeDtypeStruct((per_dev, width, inter), bf16),
-            jax.ShapeDtypeStruct((per_dev, inter, width), bf16),
+            pltpu.VMEM((rows, width), bf16),
+            pltpu.VMEM((per_dev, width, inter), bf16),
+            pltpu.VMEM((per_dev, width, inter), bf16),
+            pltpu.VMEM((per_dev, inter, width), bf16),
         ],
         in_specs=[anywhere, anywhere, in_vmem, anywhere, anywhere, anywhere, anywhere],
-        out_specs=[in_vmem, anywhere, anywhere, anywhere],
+        out_specs=[in_vmem] * 4,
         scratch_shapes=[
             pltpu.VMEM((4, rows, width), bf16),
             pltpu.VMEM((4,) + idx.shape, jnp.int32),
@@ -406,10 +417,10 @@
             pltpu.VMEM((experts, gate_rows, inter), bf16),
             pltpu.VMEM((experts, down_rows, width), bf16),
             pltpu.VMEM((plane, per_dev, gate_rows, inter), bf16),
-            pltpu.VMEM((plane, per_dev, gate_rows, inter), bf16),
             pltpu.VMEM((plane, per_dev, down_rows, width), bf16),
             pltpu.VMEM((4, rows, width), jnp.float32),
-            pltpu.VMEM((2, 2, rows, width), jnp.float32),
+            pltpu.VMEM((2, rows, width), jnp.float32),
+            pltpu.VMEM((2, rows // 2, width), jnp.float32),
             pltpu.VMEM((groups, 8, LANES), jnp.int32),
             pltpu.SMEM((groups, 8, LANES), jnp.int32),
             dma((7,)), dma((3,)), dma((3,)), dma((3,)), dma((3,)), dma((3,)), dma((groups,)), dma((groups,)), dma((2, 2, 2)), dma((2, 2, 2)),
@@ -417,9 +428,31 @@
             dma((3, 2, local, groups)), dma((3, 2, local, groups)), dma((3, 2, local, groups)), dma((3, 2, local, groups)),
             dma((2, 2, 2)), dma((2, 2, 2)), dma((3, plane)), dma((3, plane)), dma((3,)),
         ],
-        compiler_params=pltpu.CompilerParams(collective_id=0, has_side_effects=True, vmem_limit_bytes=67043328),
+        compiler_params=pltpu.CompilerParams(collective_id=0, has_side_effects=True, vmem_limit_bytes=54 * 2**20),
         name="moe_block",
     )(tokens, idx, router, table, w_gate, w_up, w_down)
+
+
+def store_kernel(*refs):
+    half = len(refs) // 2
+    copies = [pltpu.make_async_copy(refs[i], refs[half + i], refs[-1].at[i]) for i in range(half)]
+    for copy in copies:
+        copy.start()
+    for copy in copies:
+        copy.wait()
+
+
+def store_results(*results):
+    results = [pltpu.with_memory_space_constraint(x, pltpu.VMEM) for x in results]
+    return pl.pallas_call(
+        store_kernel,
+        out_shape=[jax.ShapeDtypeStruct(x.shape, x.dtype) for x in results],
+        in_specs=[pl.BlockSpec(memory_space=pltpu.VMEM)] * len(results),
+        out_specs=[pl.BlockSpec(memory_space=pl.ANY)] * len(results),
+        scratch_shapes=[pltpu.SemaphoreType.DMA((len(results),))],
+        compiler_params=pltpu.CompilerParams(vmem_limit_bytes=16 * 2**20),
+        name="store_results",
+    )(*results)
 
 
 def solution(mesh):
@@ -432,6 +465,6 @@
     def local_block(hid_rows, w_gate, w_up, w_down, w_router, slot_expert, topk_idx, topk_slot):
         table = jnp.broadcast_to(jnp.pad(slot_expert, (0, LANES - slot_expert.shape[0]))[None, :], (8, LANES))
         y_rows, p_gate, p_up, p_down = run_block(groups, members, hid_rows, topk_idx.T, w_router.T, table, w_gate, w_up, w_down, slot_expert.shape[0] // members)
-        return y_rows, p_gate, p_up, p_down
+        return store_results(y_rows, p_gate, p_up, p_down)
 
     return jax.shard_map(local_block, mesh=mesh, in_specs=(tok_spec, weight_spec, weight_spec, weight_spec, P(None, None), P("dp"), tok_spec, tok_spec), out_specs=(tok_spec, slot_spec, slot_spec, slot_spec), check_vma=False)

time: 210 us -> 203 us (0.967)
  local copies, waits for them, and re-layouts: 11.7 us -> 1.26 us
  Pallas kernels: 198 us -> 201 us
    unnamed x8 -> x0, local copies, waits for them, and re-layouts: 10.5 us -> none
    pallas_call x0 -> x1, Pallas kernels: none -> 3.94 us  [store_results(): pl.pallas_call(store_kernel, out_shape=[jax.ShapeDtypeStruct(x.shape, x.d...]
where the time goes in v5:
time: 203 us
  Pallas kernels  201 us (99%)
    pallas_call x1, Pallas kernels, run_block(): pl.pallas_call(functools.partial(block_kernel, groups, members), out_shap...  197 us

profile of v5, /device:TPU:21, one launch (start us, length us, event | category | flops | bytes accessed | tf_op | source)
XLA Modules:
  0.0 202.6 jit_solution(9528758556362461859)
XLA Ops:
  0.6 0.7 pad.4
  1.3 0.6 broadcast_in_dim.2.table_ref
  1.9 196.8 %moe_block.1 = (bf16[256,1024]{1,0:T(8,128)(2,1)S(1)}, bf16[3,1024,512]{2,1,0:T(8,128)(2,1)S(1)}, bf16[3,1024,512]{2,1,0:T(8,128)(2,1)S(1)}, bf16[3,512,1024]{2,1,0:T(8,128)(2,1)S(1)}) custom-call(bf16[256,1024]{1,0:T(8,128)(2,1)} %tok_ref.1, s32[8,256]{1,0:T(8,128)} %bitcast.3, bf16[32,1024]{1,0:T(8,128)(2,1)} %bitcast.2, ...), custom_call_target="tpu_custom_call" | custom-call | tf_op jit(solution)/shard_map/moe_block/pallas_call | solution.py:400
  198.7 3.9 %store_results.1 = (bf16[256,1024]{1,0:T(8,128)(2,1)}, bf16[3,1024,512]{2,1,0:T(8,128)(2,1)}, bf16[3,1024,512]{2,1,0:T(8,128)(2,1)}, bf16[3,512,1024]{2,1,0:T(8,128)(2,1)}) custom-call(bf16[256,1024]{1,0:T(8,128)(2,1)S(1)} %get-tuple-element.8.refs_0_, bf16[3,1024,512]{2,1,0:T(8,128)(2,1)S(1)} %get-tuple-element.9.refs_1_, ...), custom_call_target="tpu_custom_call" | custom-call | tf_op jit(solution)/shard_map/store_results/pallas_call | solution.py:447

commit v6 on v5

--- a/solution.py
+++ b/solution.py
@@ -15,7 +15,7 @@
 
 def block_kernel(groups, members, tok_ref, idx_ref, router_ref, table_ref, gate_ref, up_ref, down_ref,
                  y_ref, p_gate_ref, p_up_ref, p_down_ref,
-                 toks, idxs, gates_all, ups_all, downs_all, piece_gate, piece_up, piece_down,
+                 toks, idxs, gates_all, ups_all, downs_all, piece_gate, piece_gate_b, piece_up, piece_down,
                  send_gate, send_down, sums, sums_in, sums_mid, tables, tables_s,
                  load_sem, own_sem, early_send, early_recv, swap_send, swap_recv, table_send, table_recv, tok_send, tok_recv,
                  ring_send, ring_recv, plane_send, plane_recv, pair_send, pair_recv,
@@ -70,7 +70,8 @@
         return copy
 
     full = (gates_all, ups_all, downs_all)
-    pieces = (piece_gate, piece_up, piece_down)
+    pieces = ((piece_gate, piece_gate_b), (piece_up,) * 2, (piece_down,) * 2)
+    sizes = [weight.shape[1] // plane for weight in (gate_ref, up_ref, down_ref)]
     staged = (send_gate, send_gate, send_down)
     outs = (p_gate_ref, p_up_ref, p_down_ref)
     mine = pl.ds(core * local, local)
@@ -83,13 +84,13 @@
     ring, toked, planed, paired, summed = {}, {}, {}, {}, {}
 
     def start():
-        for i, src in enumerate((gate_ref, up_ref, down_ref)):
-            piece = pieces[i].shape[1]
-            place = pieces[i].at[block_of(0, 0, core * local, local)]
-            theirs = (q + 1 - 2 * core) * piece
-            earlies.append(send(src.at[:, pl.ds(pl.multiple_of(theirs, piece), piece), :], place, early_send.at[i], early_recv.at[i], partner))
-            owns.append(pltpu.make_async_copy(src.at[:, pl.ds(pl.multiple_of(q * piece, piece), piece), :], place, own_sem.at[i]))
-            owns[i].start()
+        for n, (i, e, src) in enumerate(((0, 0, gate_ref), (0, 1, gate_ref), (1, 0, up_ref), (2, 0, down_ref))):
+            lo, part = rows_of(i, e)
+            place = pieces[i][e].at[block_of(0, 0, core * local, local)]
+            theirs, ours = ((p * sizes[i] + lo) for p in (q + 1 - 2 * core, q))
+            earlies.append(send(src.at[:, pl.ds(pl.multiple_of(theirs, part), part), :], place, early_send.at[n], early_recv.at[n], partner))
+            owns.append(pltpu.make_async_copy(src.at[:, pl.ds(pl.multiple_of(ours, part), part), :], place, own_sem.at[n]))
+            owns[n].start()
         for i, src in enumerate((gate_ref, up_ref, down_ref)):
             swaps.append(send(src, full[i].at[mine], swap_send.at[i], swap_recv.at[i], partner))
             loads[i].start()
@@ -99,57 +100,69 @@
             swaps.append(send(table_ref, tables.at[dp], table_send.at[k], table_recv.at[k], (lax.rem(dp + k, groups), ep)))
 
     def arrived(i):
-        owns[i].wait()
-        earlies[i].wait_recv()
+        for n in (i + 1,) if i else (0, 1):
+            owns[n].wait()
+            earlies[n].wait_recv()
 
     def experts_ready():
         for i in range(3):
             loads[i].wait()
             swaps[i].wait_recv()
 
-    def tokens(hop):
-        for d in range(2):
-            if hop == 1:
-                toked[d, 1, 0] = send(tok_ref, toks.at[2 + d], tok_send.at[d, 0, 0], tok_recv.at[d, 0, 0], toward[d])
-                toked[d, 1, 1] = send(idx_ref, idxs.at[2 + d], tok_send.at[d, 0, 1], tok_recv.at[d, 0, 1], toward[d])
-            else:
-                part = pl.ds(d * half, half)
-                toked[d, 2, 0] = send(toks.at[2 + d, part], toks.at[1, part], tok_send.at[d, 1, 0], tok_recv.at[d, 1, 0], toward[d])
-                toked[d, 2, 1] = send(idxs.at[2 + d, :, part], idxs.at[1, :, part], tok_send.at[d, 1, 1], tok_recv.at[d, 1, 1], toward[d])
-
-    def tokens_near():
+    def tokens_on(d, kind, h, srcs, at):
+        part = pl.ds(h * half, half)
+        toked[d, kind, 0] = send(srcs[0].at[part], toks.at[at, part], tok_send.at[d, kind, 0], tok_recv.at[d, kind, 0], toward[d])
+        toked[d, kind, 1] = send(srcs[1].at[:, part], idxs.at[at, :, part], tok_send.at[d, kind, 1], tok_recv.at[d, kind, 1], toward[d])
+
+    def tokens_first():
+        for d in range(2):
+            tokens_on(d, 0, d, (tok_ref, idx_ref), 2 + d)
+
+    def tokens_second():
+        for d in range(2):
+            tokens_on(d, 1, 1 - d, (tok_ref, idx_ref), 2 + d)
+
+    def tokens_third():
+        tokens_here(0)
+        for d in range(2):
+            tokens_on(d, 2, d, (toks.at[2 + d], idxs.at[2 + d]), 1)
+
+    def tokens_here(kind):
         for d in range(2):
             for a in range(2):
-                toked[d, 1, a].wait_recv()
-
-    def tokens_far():
+                toked[d, kind, a].wait_recv()
+
+    def own_tokens():
         loads[3].wait()
         loads[4].wait()
-        for d in range(2):
-            for a in range(2):
-                toked[d, 2, a].wait_recv()
 
     def block_of(hop, d, lo, count):
         origin = lax.rem(z + chips - hop if d == 0 else z + hop, chips)
         return pl.ds(origin * owned + lo, count)
 
+    def share_of(i, hop, d, h, e):
+        return block_of(hop, d, h * local + e, 1) if i else block_of(hop, d, h * local, local)
+
     def pass_on(i, short, hop, e):
         for d in range(2):
             h = 1 - d if short else d
-            where = pieces[i].at[block_of(hop - 1, d, h * local + e, 1)]
+            where = pieces[i][e].at[share_of(i, hop - 1, d, h, e)]
             if hop > 1:
                 ring[i, d, h, e, hop - 1].wait_recv()
             ring[i, d, h, e, hop] = send(where, where, ring_send.at[i, d, h, e, hop - 1], ring_recv.at[i, d, h, e, hop - 1], toward[d])
 
     def rebuild(i, step, e):
-        piece = pieces[i].shape[1]
+        piece = sizes[i]
 
         def region(h, r):
             at = (other_group(r) * CORES + core) * piece
-            return (pl.ds(owned + h * local + e, 1), pl.ds(pl.multiple_of(at, piece), piece), slice(None))
+            if i:
+                return (pl.ds(owned + h * local + e, 1), pl.ds(pl.multiple_of(at, piece), piece), slice(None))
+            part = piece // local
+            return (pl.ds(owned + h * local, local), pl.ds(pl.multiple_of(at + e * part, part), part), slice(None))
 
         for h in range(2):
-            own = block_of(far, h, h * local + e, 1)
+            own = share_of(i, far, h, h, e)
             ways = bits if h == 0 else bits[::-1]
             seen, fresh = [0], [0]
             for bit in ways[:step]:
@@ -157,25 +170,26 @@
                 seen = seen + fresh
             if step == 0:
                 ring[i, h, h, e, far].wait_recv()
-                full[i][region(h, 0)] = pieces[i][own]
+                full[i][region(h, 0)] = pieces[i][e][own]
             for r in fresh:
                 if r:
                     planed[i, h, e, r].wait_recv()
-                src = full[i].at[region(h, r)] if r else pieces[i].at[own]
+                src = full[i].at[region(h, r)] if r else pieces[i][e].at[own]
                 paired[i, h, e, r] = send(src, full[i].at[region(h, r)], pair_send.at[i, h, e, r], pair_recv.at[i, h, e, r], partner)
             if step < len(ways):
                 bit = ways[step]
                 for r in seen:
-                    src = full[i].at[region(h, r)] if r else pieces[i].at[own]
+                    src = full[i].at[region(h, r)] if r else pieces[i][e].at[own]
                     planed[i, h, e, r | bit] = send(src, full[i].at[region(h, r)], plane_send.at[i, h, e, r | bit], plane_recv.at[i, h, e, r | bit], (other_group(bit), ep))
 
     def rebuilt():
         for copy in paired.values():
             copy.wait_recv()
 
-    def serve(pair, second):
-        hid = toks[2 * pair:2 * pair + 2].reshape(2 * rows, width)
-        idx = jnp.concatenate([idxs[2 * pair], idxs[2 * pair + 1]], axis=1)
+    def serve(first_block, blocks, second):
+        these = slice(first_block, first_block + blocks)
+        hid = toks[these].reshape(blocks * rows, width)
+        idx = jnp.concatenate([idxs[first_block + b] for b in range(blocks)], axis=1) if blocks > 1 else idxs[first_block]
         router = router_ref[...]
         logits = lax.dot_general(router, hid, (((1,), (1,)), ((), ())), preferred_element_type=jnp.float32)
         name = lax.broadcasted_iota(jnp.int32, logits.shape, 0)
@@ -189,7 +203,7 @@
         lane = lax.broadcasted_iota(jnp.int32, weights.shape, 1)
         first = lax.rem(z + far * second, chips) * owned
         if not second:
-            sums[2 * pair:2 * pair + 2] = jnp.zeros((2, rows, width), jnp.float32)
+            sums[these] = jnp.zeros((blocks, rows, width), jnp.float32)
 
         def expert(e, _):
             weight = jnp.sum(jnp.where(lane == first + e, weights, 0.0), axis=1, keepdims=True)
@@ -199,22 +213,26 @@
             hidden_act = (jax.nn.silu(act_a) * act_b).astype(jnp.bfloat16)
             expert_out = jnp.dot(hidden_act, downs_all[at], preferred_element_type=jnp.float32)
             contrib = jnp.where(weight < 0.0, 0.0, weight * expert_out.astype(jnp.bfloat16).astype(jnp.float32))
-            sums[2 * pair:2 * pair + 2] += contrib.reshape(2, rows, width)
+            sums[these] += contrib.reshape(blocks, rows, width)
             return 0
 
         lax.fori_loop(0, owned, expert, 0)
 
-    def slot_copy(i, k):
-        piece = pieces[i].shape[1]
-        place = pl.ds(pl.multiple_of(q * piece, piece), piece)
+    def rows_of(i, e):
+        part = sizes[i] // (1 if i else local)
+        return e * part, part
+
+    def slot_copy(i, e, k):
+        lo, part = rows_of(i, e)
+        place = pl.ds(pl.multiple_of(q * sizes[i] + lo, part), part)
         return pltpu.make_async_remote_copy(
-            src_ref=staged[i].at[k], dst_ref=outs[i].at[:, place, :], send_sem=slot_send.at[i, k], recv_sem=slot_recv.at[i, k],
-            device_id=plane_device(k), device_id_type=MESH)
-
-    def slot_copy_own(i):
-        piece = pieces[i].shape[1]
-        place = pl.ds(pl.multiple_of(q * piece, piece), piece)
-        return pltpu.make_async_copy(staged[i].at[0], outs[i].at[:, place, :], slot_own.at[i])
+            src_ref=staged[i].at[k, :, pl.ds(lo, part)], dst_ref=outs[i].at[:, place, :],
+            send_sem=slot_send.at[3 * e + i, k], recv_sem=slot_recv.at[3 * e + i, k], device_id=plane_device(k), device_id_type=MESH)
+
+    def slot_copy_own(i, e):
+        lo, part = rows_of(i, e)
+        place = pl.ds(pl.multiple_of(q * sizes[i] + lo, part), part)
+        return pltpu.make_async_copy(staged[i].at[0, :, pl.ds(lo, part)], outs[i].at[:, place, :], slot_own.at[3 * e + i])
 
     def tables_ready():
         loads[5].wait()
@@ -224,38 +242,40 @@
         load.start()
         load.wait()
 
-    def exchange(i):
-        for d in range(2):
-            for e in range(local):
-                ring[i, d, 1 - d, e, far - 1].wait_recv()
+    def exchange(i, e):
+        for d in range(2):
+            for share in range(local) if i else (e,):
+                ring[i, d, 1 - d, share, far - 1].wait_recv()
+        lo, part = rows_of(i, e)
 
         def pick(k, _):
             group, member = plane_device(k)
             for s in range(slots):
-                staged[i][k, s] = pieces[i][tables_s[group, 0, member * slots + s]]
+                staged[i][k, s, lo:lo + part] = pieces[i][e][tables_s[group, 0, member * slots + s]]
             return 0
 
         def begin(k, _):
-            slot_copy(i, k).start()
+            slot_copy(i, e, k).start()
             return 0
 
         if i == 1:
-            left(0)
+            left(0, 0)
+            left(0, 1)
         lax.fori_loop(0, plane, pick, 0)
         lax.fori_loop(1, plane, begin, 0)
-        slot_copy_own(i).start()
-
-    def left(i):
+        slot_copy_own(i, e).start()
+
+    def left(i, e):
         def wait(k, _):
-            slot_copy(i, k).wait_send()
+            slot_copy(i, e, k).wait_send()
             return 0
 
         lax.fori_loop(1, plane, wait, 0)
-        slot_copy_own(i).wait()
-
-    def landed(i):
+        slot_copy_own(i, e).wait()
+
+    def landed(i, e):
         def wait(k, _):
-            slot_copy(i, k).wait_recv()
+            slot_copy(i, e, k).wait_recv()
             return 0
 
         lax.fori_loop(1, plane, wait, 0)
@@ -288,100 +308,105 @@
     start()
     arrived(gate)
     pass_on(gate, long, 1, 0)
+    pass_on(gate, short, 1, 0)
+    pass_on(gate, long, 2, 0)
+    pass_on(gate, short, 2, 0)
+    pass_on(gate, long, 3, 0)
     pass_on(gate, long, 1, 1)
-    pass_on(gate, long, 2, 0)
-    pass_on(gate, long, 2, 1)
-    pass_on(gate, short, 1, 0)
-    pass_on(gate, long, 3, 1)
-    pass_on(gate, long, 3, 0)
+    pass_on(gate, long, 4, 0)
+    pass_on(gate, short, 3, 0)
     pass_on(gate, short, 1, 1)
-    pass_on(gate, long, 4, 1)
-    pass_on(gate, long, 4, 0)
-    pass_on(gate, short, 2, 1)
-    rebuild(gate, 0, 1)
-    pass_on(gate, short, 2, 0)
     rebuild(gate, 0, 0)
-    pass_on(gate, short, 3, 1)
-    rebuild(gate, 1, 1)
-    pass_on(gate, short, 3, 0)
-    rebuild(gate, 1, 0)
     arrived(down)
     pass_on(down, long, 1, 1)
+    tables_ready()
+    exchange(gate, 0)
+    pass_on(gate, long, 2, 1)
+    pass_on(gate, short, 2, 1)
+    pass_on(down, long, 2, 1)
+    pass_on(gate, long, 3, 1)
+    pass_on(gate, short, 3, 1)
+    pass_on(gate, long, 4, 1)
+    arrived(up)
+    pass_on(up, long, 1, 0)
+    rebuild(gate, 1, 0)
+    pass_on(down, long, 3, 1)
+    rebuild(gate, 0, 1)
     pass_on(down, long, 1, 0)
-    arrived(up)
+    exchange(gate, 1)
+    pass_on(down, long, 4, 1)
+    for step in range(2, last + 1):
+        rebuild(gate, step, 0)
+    pass_on(down, long, 2, 0)
     pass_on(up, long, 1, 1)
-    tables_ready()
-    exchange(gate)
-    pass_on(down, long, 2, 1)
-    pass_on(up, long, 1, 0)
+    pass_on(down, long, 3, 0)
+    pass_on(up, long, 2, 0)
+    pass_on(down, long, 4, 0)
+    rebuild(down, 0, 1)
     pass_on(up, long, 2, 1)
-    pass_on(up, long, 2, 0)
+    pass_on(up, long, 3, 0)
+    rebuild(gate, 1, 1)
+    rebuild(down, 0, 0)
     pass_on(up, long, 3, 1)
-    pass_on(up, long, 3, 0)
+    pass_on(up, long, 4, 0)
+    pass_on(up, short, 1, 1)
+    rebuild(down, 1, 1)
     pass_on(up, long, 4, 1)
+    pass_on(up, short, 1, 0)
+    rebuild(up, 0, 0)
+    pass_on(up, short, 2, 1)
+    rebuild(down, 1, 0)
+    rebuild(up, 0, 1)
+    pass_on(up, short, 2, 0)
+    rebuild(up, 1, 0)
+    for step in range(2, last + 1):
+        rebuild(down, step, 1)
+    pass_on(up, short, 3, 1)
+    pass_on(up, short, 3, 0)
+    rebuild(up, 1, 1)
+    pass_on(down, short, 1, 0)
+    tokens_first()
     for step in range(2, last + 1):
         rebuild(gate, step, 1)
-    pass_on(down, long, 2, 0)
-    pass_on(up, long, 4, 0)
-    pass_on(down, long, 3, 1)
-    pass_on(down, long, 3, 0)
-    rebuild(up, 0, 1)
-    for step in range(2, last + 1):
-        rebuild(gate, step, 0)
-    rebuild(up, 0, 0)
-    pass_on(up, short, 1, 0)
-    pass_on(up, short, 1, 1)
-    pass_on(down, long, 4, 0)
-    rebuild(up, 1, 1)
-    pass_on(up, short, 2, 0)
-    pass_on(down, long, 4, 1)
-    rebuild(down, 0, 0)
-    pass_on(up, short, 2, 1)
-    pass_on(up, short, 3, 0)
-    rebuild(up, 1, 0)
-    pass_on(up, short, 3, 1)
-    rebuild(down, 0, 1)
-    tokens(1)
-    rebuild(down, 1, 0)
-    rebuild(down, 1, 1)
+    tokens_second()
+    exchange(up, 0)
+    pass_on(down, short, 2, 0)
+    experts_ready()
+    own_tokens()
+    serve(0, 1, 0)
+    for step in range(2, last + 1):
+        rebuild(down, step, 0)
+    for step in range(2, last + 1):
+        rebuild(up, step, 1)
     pass_on(down, short, 1, 1)
+    tokens_third()
+    tokens_here(1)
+    serve(2, 2, 0)
+    pass_on(down, short, 2, 1)
+    pass_on(down, short, 3, 0)
     for step in range(2, last + 1):
         rebuild(up, step, 0)
-    exchange(up)
-    for step in range(2, last + 1):
-        rebuild(down, step, 0)
-    pass_on(down, short, 1, 0)
-    tokens_near()
-    tokens(2)
-    experts_ready()
-    serve(1, 0)
-    pass_on(down, short, 2, 0)
-    for step in range(2, last + 1):
-        rebuild(up, step, 1)
-    for step in range(2, last + 1):
-        rebuild(down, step, 1)
-    pass_on(down, short, 2, 1)
-    tokens_far()
-    serve(0, 0)
-    pass_on(down, short, 3, 0)
+    tokens_here(2)
+    serve(1, 1, 0)
     pass_on(down, short, 3, 1)
     rebuilt()
-    serve(0, 1)
+    serve(1, 1, 1)
     sums_far()
-    exchange(down)
-    serve(1, 1)
+    exchange(down, 0)
+    serve(2, 2, 1)
     sums_near()
     sums_joined()
+    serve(0, 1, 1)
     for d in range(2):
         for h in range(2):
             summed[d, 1, h].wait_recv()
     y_ref[...] = (sums[0] + sums_in[0] + sums_in[1]).astype(jnp.bfloat16)
     for copy in sent:
         copy.wait_send()
-    left(1)
-    left(2)
-    for i in range(3):
-        landed(i)
+    left(1, 0)
+    left(2, 0)
+    for i, e in ((0, 0), (0, 1), (1, 0), (2, 0)):
+        landed(i, e)
 
 
 def run_block(groups, members, tokens, idx, router, table, w_gate, w_up, w_down, per_dev):
@@ -413,7 +438,8 @@
             pltpu.VMEM((2 * owned, width, inter), bf16),
             pltpu.VMEM((2 * owned, width, inter), bf16),
             pltpu.VMEM((2 * owned, inter, width), bf16),
-            pltpu.VMEM((experts, gate_rows, inter), bf16),
+            pltpu.VMEM((experts, gate_rows // local, inter), bf16),
+            pltpu.VMEM((experts, gate_rows // local, inter), bf16),
             pltpu.VMEM((experts, gate_rows, inter), bf16),
             pltpu.VMEM((experts, down_rows, width), bf16),
             pltpu.VMEM((plane, per_dev, gate_rows, inter), bf16),
@@ -423,10 +449,10 @@
             pltpu.VMEM((2, rows // 2, width), jnp.float32),
             pltpu.VMEM((groups, 8, LANES), jnp.int32),
             pltpu.SMEM((groups, 8, LANES), jnp.int32),
-            dma((7,)), dma((3,)), dma((3,)), dma((3,)), dma((3,)), dma((3,)), dma((groups,)), dma((groups,)), dma((2, 2, 2)), dma((2, 2, 2)),
+            dma((7,)), dma((4,)), dma((4,)), dma((4,)), dma((3,)), dma((3,)), dma((groups,)), dma((groups,)), dma((2, 3, 2)), dma((2, 3, 2)),
             dma((3, 2, 2, local, far)), dma((3, 2, 2, local, far)),
             dma((3, 2, local, groups)), dma((3, 2, local, groups)), dma((3, 2, local, groups)), dma((3, 2, local, groups)),
-            dma((2, 2, 2)), dma((2, 2, 2)), dma((3, plane)), dma((3, plane)), dma((3,)),
+            dma((2, 2, 2)), dma((2, 2, 2)), dma((4, plane)), dma((4, plane)), dma((4,)),
         ],
         compiler_params=pltpu.CompilerParams(collective_id=0, has_side_effects=True, vmem_limit_bytes=54 * 2**20),
         name="moe_block",

time: 203 us -> 199 us (0.980)
  Pallas kernels: 201 us -> 196 us
    pallas_call x1, Pallas kernels: 197 us -> 192 us  [run_block(): pl.pallas_call(functools.partial(block_kernel, groups, members), out_shap...]
where the time goes in v6:
time: 199 us; the launch traced here: 198 us
  Pallas kernels  196 us (98%)
    pallas_call x1, Pallas kernels, run_block(): pl.pallas_call(functools.partial(block_kernel, groups, members), out_shap...  192 us

profile of v6, /device:TPU:21, one launch (start us, length us, event | category | flops | bytes accessed | tf_op | source)
XLA Modules:
  0.0 197.7 jit_solution(8107279755340401721)
XLA Ops:
  0.6 0.7 pad.4
  1.3 0.6 broadcast_in_dim.2.table_ref
  1.9 191.8 %moe_block.1 = (bf16[256,1024]{1,0:T(8,128)(2,1)S(1)}, bf16[3,1024,512]{2,1,0:T(8,128)(2,1)S(1)}, bf16[3,1024,512]{2,1,0:T(8,128)(2,1)S(1)}, bf16[3,512,1024]{2,1,0:T(8,128)(2,1)S(1)}) custom-call(bf16[256,1024]{1,0:T(8,128)(2,1)} %tok_ref.1, s32[8,256]{1,0:T(8,128)} %bitcast.3, bf16[32,1024]{1,0:T(8,128)(2,1)} %bitcast.2, ...), custom_call_target="tpu_custom_call" | custom-call | tf_op jit(solution)/shard_map/moe_block/pallas_call | solution.py:425
  193.7 3.9 %store_results.1 = (bf16[256,1024]{1,0:T(8,128)(2,1)}, bf16[3,1024,512]{2,1,0:T(8,128)(2,1)}, bf16[3,1024,512]{2,1,0:T(8,128)(2,1)}, bf16[3,512,1024]{2,1,0:T(8,128)(2,1)}) custom-call(bf16[256,1024]{1,0:T(8,128)(2,1)S(1)} %get-tuple-element.8.refs_0_, bf16[3,1024,512]{2,1,0:T(8,128)(2,1)S(1)} %get-tuple-element.9.refs_1_, ...), custom_call_target="tpu_custom_call" | custom-call | tf_op jit(solution)/shard_map/store_results/pallas_call | solution.py:473

commit v7 on v6

--- a/solution.py
+++ b/solution.py
@@ -489,7 +489,7 @@
     slot_spec = P(("dp", "ep"), None, None)
 
     def local_block(hid_rows, w_gate, w_up, w_down, w_router, slot_expert, topk_idx, topk_slot):
-        table = jnp.broadcast_to(jnp.pad(slot_expert, (0, LANES - slot_expert.shape[0]))[None, :], (8, LANES))
+        table = jnp.pad(slot_expert[None, :], ((0, 7), (0, LANES - slot_expert.shape[0])))
         y_rows, p_gate, p_up, p_down = run_block(groups, members, hid_rows, topk_idx.T, w_router.T, table, w_gate, w_up, w_down, slot_expert.shape[0] // members)
         return store_results(y_rows, p_gate, p_up, p_down)
 

time: 199 us -> 199 us (level)
  no operation moved by 1% of the time
where the time goes in v7:
time: 199 us; the launch traced here: 198 us
  Pallas kernels  196 us (98%)
    pallas_call x1, Pallas kernels, run_block(): pl.pallas_call(functools.partial(block_kernel, groups, members), out_shap...  192 us

profile of v7, /device:TPU:21, one launch (start us, length us, event | category | flops | bytes accessed | tf_op | source)
XLA Modules:
  0.0 197.7 jit_solution(11642180440271697847)
XLA Ops:
  0.6 1.3 pad.4.table_ref
  1.9 191.8 %moe_block.1 = (bf16[256,1024]{1,0:T(8,128)(2,1)S(1)}, bf16[3,1024,512]{2,1,0:T(8,128)(2,1)S(1)}, bf16[3,1024,512]{2,1,0:T(8,128)(2,1)S(1)}, bf16[3,512,1024]{2,1,0:T(8,128)(2,1)S(1)}) custom-call(bf16[256,1024]{1,0:T(8,128)(2,1)} %tok_ref.1, s32[8,256]{1,0:T(8,128)} %bitcast.4, bf16[32,1024]{1,0:T(8,128)(2,1)} %bitcast.3, s32[8,128]{1,0:T(8,128)} %pad.4.table_ref, ...), custom_call_target="tpu_custom_call" | custom-call | tf_op jit(solution)/shard_map/moe_block/pallas_call | solution.py:425
  193.7 3.9 %store_results.1 = (bf16[256,1024]{1,0:T(8,128)(2,1)}, bf16[3,1024,512]{2,1,0:T(8,128)(2,1)}, bf16[3,1024,512]{2,1,0:T(8,128)(2,1)}, bf16[3,512,1024]{2,1,0:T(8,128)(2,1)}) custom-call(bf16[256,1024]{1,0:T(8,128)(2,1)S(1)} %get-tuple-element.8.refs_0_, bf16[3,1024,512]{2,1,0:T(8,128)(2,1)S(1)} %get-tuple-element.9.refs_1_, ...), custom_call_target="tpu_custom_call" | custom-call | tf_op jit(solution)/shard_map/store_results/pallas_call | solution.py:473
